TPU v7x, 32 devices: a whole 2x2x4 slice. The times are simulated.
32 devices in a mesh: lev: 4 (over z), wav: 8 (over y, x, core).
Axes of the slice: x: 2, y: 2, z: 4, core: 2. Of those that a mesh axis runs over, the one named last changes fastest.
Arguments:
- grid_field: float32 [8, 1216, 1216], P('lev', 'wav'), may hold values from -6 to 6
- truncation_limit: int32 [1216], replicated, may hold values from -1 to 607, as said below
- diffusion_order: int32 [8], P('lev'), may hold values from 1 to 4
- diffusion_strength: float32 [8], P('lev'), may hold values from 2 to 50
- mass_weight: float32 [8], P('lev'), may hold values from 0.25 to 4
Outputs:
- filtered: float32 [8, 1216, 1216], P('lev', 'wav')
- energies: float32 [8], P('lev')
- total_energy: float32 [], replicated
Inputs may be any that keep to these rules, and one draw needn't show every extreme that they name: `truncation_limit`: the largest |wavenumber(q)| kept at index p, with wavenumber(m) = m below 608 and m - 1216 otherwise; the kept set is an ellipse about wavenumber zero; the value at p equals the value at 1216 - p; -1 where nothing is kept; the value at p = 0 is 607.
All inputs are finite; a program needn't handle non-finite values.
Results may differ from a plain program's by a relative error of at most 0.000071.
Values sent between devices are 32-bit elements.
A program may use at most 64 MiB of HBM per device.

v0:
```python
import functools

import jax
import jax.numpy as jnp
import numpy as np
from jax import lax
from jax.experimental import pallas as pl
from jax.experimental.pallas import tpu as pltpu
from jax.sharding import PartitionSpec as P

product_precision = lax.Precision.HIGH


def tables(length):
    step = 32
    coarse = -(-length // step)
    columns = np.arange(length)
    high = 2.0 * np.pi / length * (np.arange(coarse)[:, None] * step * columns[None, :] % length)
    low = 2.0 * np.pi / length * (np.arange(step)[:, None] * columns[None, :] % length)
    cos_high, sin_high = (jnp.asarray(f(high), jnp.float32)[:, None] for f in (np.cos, np.sin))
    cos_low, sin_low = (jnp.asarray(f(low), jnp.float32)[None] for f in (np.cos, np.sin))
    cosine = cos_high * cos_low - sin_high * sin_low
    sine = sin_high * cos_low + cos_high * sin_low
    return tuple(t.reshape(coarse * step, length)[:length] for t in (cosine, sine))


def signed(positions, length):
    return jnp.where(positions < length // 2, positions, positions - length)


def transform(values, cosine_table, sine_table, direction):
    with_cosine = jnp.einsum("scpi,iq->scpq", values, cosine_table, precision=product_precision)
    with_sine = jnp.einsum("scpi,iq->scpq", values, sine_table, precision=product_precision)
    if direction < 0:
        real_part = with_cosine[:, 0] + with_sine[:, 1]
        imaginary = with_cosine[:, 1] - with_sine[:, 0]
    else:
        real_part = with_cosine[:, 0] - with_sine[:, 1]
        imaginary = with_cosine[:, 1] + with_sine[:, 0]
    return jnp.stack([real_part, imaginary], axis=1)


def damping(wave_rows, limits, length, diffusion_order, diffusion_strength):
    wave_first = signed(jnp.arange(length, dtype=jnp.int32), length)
    rows_float = wave_rows.astype(jnp.float32)
    first_float = wave_first.astype(jnp.float32)
    scaled_radius = (rows_float[:, None] ** 2 + first_float[None, :] ** 2) / (0.5 * length) ** 2
    inside = (jnp.abs(wave_first)[None, :] <= limits[:, None]).astype(jnp.float32)
    powered = jnp.power(scaled_radius[None], diffusion_order.astype(jnp.float32)[:, None, None])
    return inside[None] / (1.0 + diffusion_strength[:, None, None] * powered)


def mirrored(values):
    return jnp.roll(jnp.flip(values, -1), 1, -1)


def half_plane(
    grid_field, truncation_limit, diffusion_order, diffusion_strength, cosine_table, sine_table
):
    length = grid_field.shape[2]
    half = length // 2
    row_real = jnp.einsum("sij,jl->sli", grid_field, cosine_table[:, :half], precision=product_precision)
    row_imag = -jnp.einsum("sij,jl->sli", grid_field, sine_table[:, :half], precision=product_precision)
    nyquist = jnp.einsum("sij,j->si", grid_field, cosine_table[:, half], precision=product_precision)
    zero_row = (jnp.arange(half, dtype=jnp.int32) == 0)[None, :, None]
    row_imag = jnp.where(zero_row, nyquist[:, None, :], row_imag)
    along_rows = jnp.stack([row_real, row_imag], axis=1)
    spectrum = transform(
        lax.all_to_all(along_rows, "wav", split_axis=2, concat_axis=3, tiled=True),
        cosine_table,
        sine_table,
        -1,
    )
    column_count = spectrum.shape[2]
    wav_index = lax.axis_index("wav")
    offset = wav_index * column_count
    wave_rows = offset + jnp.arange(column_count, dtype=jnp.int32)
    limits = lax.dynamic_slice(truncation_limit, (offset,), (column_count,))
    damp_main = damping(wave_rows, limits, length, diffusion_order, diffusion_strength)
    nyquist_rows = signed(jnp.full((1,), half, jnp.int32), length)
    damp_top = damping(
        nyquist_rows, truncation_limit[half : half + 1], length, diffusion_order, diffusion_strength
    )[:, 0]
    damped = spectrum * damp_main[:, None]
    packed_real = spectrum[:, 0, 0, :]
    packed_imag = spectrum[:, 1, 0, :]
    back_real = mirrored(packed_real)
    back_imag = mirrored(packed_imag)
    zero_real = (packed_real + back_real) * 0.5 * damp_main[:, 0]
    zero_imag = (packed_imag - back_imag) * 0.5 * damp_main[:, 0]
    top_real = (packed_imag + back_imag) * 0.5 * damp_top
    top_imag = (back_real - packed_real) * 0.5 * damp_top
    is_zero = wave_rows == 0
    column_weight = jnp.where(is_zero, 0.0, 2.0).astype(jnp.float32)
    edge = jnp.sum(zero_real**2 + zero_imag**2 + top_real**2 + top_imag**2, axis=-1)
    main_sum = jnp.sum(damped * damped * column_weight[None, None, :, None], axis=(1, 2, 3))
    partial_value = (main_sum + jnp.where(wav_index == 0, edge, 0.0)) / float(length) ** 4
    zero_column = is_zero[None, :, None]
    repacked = jnp.stack(
        [
            jnp.where(zero_column, (zero_real - top_imag)[:, None, :], damped[:, 0]),
            jnp.where(zero_column, (zero_imag + top_real)[:, None, :], damped[:, 1]),
        ],
        axis=1,
    )
    along_first = transform(repacked, cosine_table, sine_table, 1)
    inverse_area = 1.0 / float(length) ** 2
    received = lax.all_to_all(along_first, "wav", split_axis=3, concat_axis=2, tiled=True)
    row_weight = jnp.where(jnp.arange(half, dtype=jnp.int32) == 0, 1.0, 2.0).astype(jnp.float32)[
        :, None
    ]
    with_cosine = jnp.einsum(
        "spi,pj->sij", received[:, 0] * row_weight, cosine_table[:half], precision=product_precision
    )
    with_sine = jnp.einsum(
        "spi,pj->sij", received[:, 1] * row_weight, sine_table[:half], precision=product_precision
    )
    top_term = received[:, 1, 0, :][:, :, None] * cosine_table[half][None, None, :]
    filtered = (with_cosine - with_sine + top_term) * inverse_area
    return (filtered, partial_value)


LANES = 128
HALF = LANES // 2
MESH = pl.DeviceIdType.MESH


def halves(values):
    high = values.astype(jnp.bfloat16)
    return high, (values - high.astype(jnp.float32)).astype(jnp.bfloat16)


def product(left, right):
    dot = functools.partial(jnp.dot, preferred_element_type=jnp.float32)
    return dot(left[0], right[0]) + dot(left[1], right[0]) + dot(left[0], right[1])


def swap(value):
    count = value.shape[1] // LANES
    turned = [pltpu.roll(value[:, n * LANES : (n + 1) * LANES], HALF, 1) for n in range(count)]
    return jnp.concatenate(turned, 1) if count > 1 else turned[0]


def eight_points(x, sign, signs):
    turn = signs if sign < 0 else -signs

    def four(p, q, r, t):
        a0, a1, a2, a3 = p + r, p - r, q + t, swap(q - t) * turn
        return a0 + a2, a1 + a3, a0 - a2, a1 - a3

    e = four(x[0], x[2], x[4], x[6])
    o = four(x[1], x[3], x[5], x[7])
    root = 0.5**0.5
    odd = (
        o[0],
        root * (o[1] + swap(o[1]) * turn),
        swap(o[2]) * turn,
        root * (swap(o[3]) * turn - o[3]),
    )
    return [e[n] + odd[n] for n in range(4)] + [e[n] - odd[n] for n in range(4)]


def pieces(rows, group_rows, groups):
    found = []
    for group in range(groups):
        start, stop = group * group_rows, min((group + 1) * group_rows, 2 * rows)
        while start < stop:
            part = start // rows
            end = min(stop, (part + 1) * rows)
            found.append((group, start - group * group_rows, part, start - part * rows, end - start))
            start = end
    return found


def fused_kernel(
    sizes,
    grid_ref, limit_ref, order_ref, strength_ref, mass_ref, coarse_ref, fine_ref,
    back_coarse_hbm, back_fine_hbm, twiddle_hbm, base_hbm,
    out_ref, energy_ref, total_ref,
    grid_parts, table, back_table, back_coarse, back_fine, twiddle, base,
    sent_a, got_a, sent_b, got_b, back_a, home_a, back_b, home_b,
    rest, work, damp, energy_mine, energy_all,
    load_sems, send_sems, recv_sems, e_send_sems, e_recv_sems, local_sems,
):
    slabs, rows, length, wav, lev, quarters, columns, padded, tail, groups, group_rows, fine_rows = sizes
    everyone = lev * wav
    half = length // 2
    me = lax.axis_index("wav")
    level = lax.axis_index("lev")
    my_quarter, my_slab = me // slabs, me % slabs
    flat = level * wav + me

    barrier = pltpu.get_barrier_semaphore()

    @pl.loop(1, everyone)
    def _(step):
        target = (flat + step) % everyone
        pl.semaphore_signal(barrier, inc=1, device_id=(target // wav, target % wav), device_id_type=MESH)

    loads = [
        pltpu.make_async_copy(src, dst, load_sems.at[n])
        for n, (src, dst) in enumerate(
            ((twiddle_hbm, twiddle), (base_hbm, base), (back_coarse_hbm, back_coarse), (back_fine_hbm, back_fine))
        )
    ]
    for load in loads:
        load.start()
    high, low = halves(grid_ref[...])
    grid_parts[0] = high
    grid_parts[1] = low

    def quarter_of(step):
        down, across = 1 - step % 2, 1 - step // 2
        y, x = my_quarter // 2, my_quarter % 2
        return (y + down - 2 * y * down) * 2 + (x + across - 2 * x * across)

    def push(source, target, phase, w):
        @pl.when(w != me)
        def _():
            pltpu.make_async_remote_copy(
                src_ref=source.at[w], dst_ref=target.at[me],
                send_sem=send_sems.at[phase, w], recv_sem=recv_sems.at[phase, me],
                device_id=(level, w), device_id_type=MESH,
            ).start()

        @pl.when(w == me)
        def _():
            pltpu.make_async_copy(source.at[w], target.at[w], local_sems.at[phase]).start()

    def arrive(source, target, phase, w):
        @pl.when(w != me)
        def _():
            pltpu.make_async_remote_copy(
                src_ref=source.at[w], dst_ref=target.at[w],
                send_sem=send_sems.at[phase, w], recv_sem=recv_sems.at[phase, w],
                device_id=(level, w), device_id_type=MESH,
            ).wait()

        @pl.when(w == me)
        def _():
            pltpu.make_async_copy(source.at[w], target.at[w], local_sems.at[phase]).wait()

    lane = lax.broadcasted_iota(jnp.int32, (1, LANES), 1)
    signs = jnp.where(lane < HALF, 1.0, -1.0)
    in_part = [(lane >= part * HALF) & (lane < part * HALF + tail) for part in range(2)]
    layout = pieces(rows, group_rows, groups)

    def pack(tile):
        shifted = {}
        for group, at, part, start, count in layout:
            piece = jnp.where(in_part[part], tile(start, count), 0.0)
            shift = (group * tail - part * HALF) % LANES
            shifted.setdefault(group, []).append(pltpu.roll(piece, shift, 1) if shift else piece)
        packed = jnp.zeros((group_rows, LANES), jnp.float32)
        for found in shifted.values():
            whole = jnp.concatenate(found, 0) if len(found) > 1 else found[0]
            if whole.shape[0] < group_rows:
                fill = jnp.zeros((group_rows - whole.shape[0], LANES), jnp.float32)
                whole = jnp.concatenate([whole, fill], 0)
            packed = packed + whole
        return packed

    def unpack(packed):
        found = {0: [], 1: []}
        for group, at, part, start, count in layout:
            piece = packed[at : at + count]
            shift = (part * HALF - group * tail) % LANES
            piece = pltpu.roll(piece, shift, 1) if shift else piece
            found[part].append(jnp.where(in_part[part], piece, 0.0))
        return jnp.concatenate(found[0], 0) + jnp.concatenate(found[1], 0)

    def forward(first, count, phase, source, target):
        @pl.loop(0, quarters)
        def _(step):
            quarter = quarter_of(step)
            columns_of = slice(first * LANES, (first + count) * LANES)
            cos_f, sin_f = fine_ref[0, quarter, :, columns_of], fine_ref[1, quarter, :, columns_of]

            @pl.loop(0, length // fine_rows, unroll=2)
            def _(block):
                cos_c = coarse_ref[0, quarter, pl.ds(block, 1)][:, columns_of]
                sin_c = coarse_ref[1, quarter, pl.ds(block, 1)][:, columns_of]
                span = pl.ds(pl.multiple_of(block * fine_rows, fine_rows), fine_rows)
                value_high, value_low = halves(cos_c * cos_f - sin_c * sin_f)
                table[0, span, : count * LANES] = value_high
                table[1, span, : count * LANES] = value_low

            result = product(
                (grid_parts[0], grid_parts[1]), (table[0, :, : count * LANES], table[1, :, : count * LANES])
            )
            for slab in range(slabs):
                w = quarter * slabs + slab
                source[w, :rows] = result[slab * rows : (slab + 1) * rows, :LANES]
                if count > 1:
                    source[w, rows:] = pack(
                        lambda start, many: result[slab * rows + start : slab * rows + start + many, LANES:]
                    )

            if first == 0:
                @pl.when(step == 0)
                def _():
                    pl.semaphore_wait(barrier, everyone - 1)

            for slab in range(slabs):
                push(source, target, phase, quarter * slabs + slab)

    forward(0, 1, 0, sent_a, got_a)
    forward(1, 2, 1, sent_b, got_b)

    loads[0].wait()
    loads[1].wait()
    place = lax.broadcasted_iota(jnp.int32, (1, 3 * LANES), 1)
    column = place // LANES * HALF + place % HALF
    wave = my_quarter * columns + column
    valid = (column < columns) | ((column == columns) & (wave == half))
    single = (wave == 0) | (wave == half)
    out_weight = jnp.where(single, 1.0, 2.0) / float(length) ** 2
    energy_weight = jnp.where(single, 1.0, 0.5)
    all_limits = limit_ref[...]
    limits = jnp.full((1, 3 * LANES), -1, jnp.int32)
    for quarter in range(quarters):
        found = []
        for tile in range(3):
            start = quarter * columns + tile * HALF
            found += [all_limits[:, start : start + HALF]] * 2
        limits = jnp.where(my_quarter == quarter, jnp.concatenate(found, 1), limits)
    limits = jnp.where(valid, limits, -1)
    order = order_ref[my_slab]
    strength = strength_ref[my_slab]
    wave_square = wave.astype(jnp.float32) ** 2

    @pl.loop(0, wav)
    def _(m):
        row = lax.broadcasted_iota(jnp.int32, (padded, 1), 0)
        q = row * wav + m
        signed_q = jnp.where(q < half, q, q - length)
        radius = (wave_square + signed_q.astype(jnp.float32) ** 2) / (0.5 * length) ** 2
        square = radius * radius
        powered = jnp.where(order >= 3, square, 1.0) * jnp.where(order % 2 == 1, radius, square)
        inside = (jnp.abs(signed_q) <= limits) & (row < rows)
        damp[m] = jnp.where(inside, out_weight / (1.0 + strength * powered), 0.0)
        work[m, rows:] = jnp.zeros((padded - rows, 2 * LANES), jnp.float32)

    def along(value):
        value_high, value_low = halves(value)
        stacked = jnp.concatenate([value_high, value_high, value_low], 0)
        return jnp.dot(base[...], stacked, preferred_element_type=jnp.float32)

    block_rows = 24

    def in_blocks(body):
        @pl.loop(0, rows // block_rows)
        def _(block):
            body(pl.multiple_of(block * block_rows, 8), block_rows)

        if rows % block_rows:
            body(rows - rows % block_rows, rows % block_rows)

    def middle(first, count, phase, got, back, home, announce):
        spans = slice(0, count * LANES)
        all_signs = jnp.concatenate([signs] * count, 1)

        def split(start, many):
            span = pl.ds(start, many)
            for tile in range(count):
                x = [rest[w, span] if tile else got[w, span] for w in range(wav)]
                for m, value in enumerate(eight_points(x, -1, signs)):
                    work[m, span, tile * LANES : (tile + 1) * LANES] = value

        in_blocks(split)

        def one_residue(m, sums):
            packed_turn = twiddle[m]
            other_turn = swap(packed_turn)
            cos_t = jnp.concatenate([jnp.where(lane < HALF, packed_turn, other_turn)] * count, 1)
            sin_t = jnp.concatenate([jnp.where(lane < HALF, other_turn, -packed_turn)] * count, 1)
            value = work[m, :, spans]
            both = along(value * cos_t + swap(value) * sin_t)
            value = both[:padded] + swap(both[padded:]) * all_signs
            value = value * damp[m, :, first * LANES : (first + count) * LANES]
            sums = sums + jnp.sum((value * value).reshape(padded // 8, 8, count * LANES), axis=0)
            both = along(value)
            value = both[:padded] - swap(both[padded:]) * all_signs
            work[m, :, spans] = value * cos_t - swap(value) * sin_t
            return sums

        sums = jnp.zeros((8, count * LANES), jnp.float32)
        for m in range(wav):
            sums = one_residue(m, sums)
        sums = sums * energy_weight[:, first * LANES : (first + count) * LANES]

        announce(sum(sums[:, n * LANES : (n + 1) * LANES] for n in range(count)))

        def join(start, many):
            span = pl.ds(start, many)
            for tile in range(count):
                v = [work[m, span, tile * LANES : (tile + 1) * LANES] for m in range(wav)]
                for w, value in enumerate(eight_points(v, 1, signs)):
                    if tile:
                        rest[w, span] = value
                    else:
                        back[w, span] = value

        in_blocks(join)

        @pl.loop(0, quarters)
        def _(step):
            for slab in range(slabs):
                w = quarter_of(step) * slabs + slab
                if count > 1:
                    back[w, rows:] = pack(lambda start, many: rest[w, start : start + many])
                push(back, home, phase, w)

    @pl.loop(0, wav)
    def _(w):
        arrive(sent_a, got_a, 0, w)

    def energy_copy(target_flat, slot):
        return pltpu.make_async_remote_copy(
            src_ref=energy_mine, dst_ref=energy_all.at[slot],
            send_sem=e_send_sems.at[target_flat], recv_sem=e_recv_sems.at[slot],
            device_id=(target_flat // wav, target_flat % wav), device_id_type=MESH,
        )

    def announce_first(sums):
        energy_mine[0] = sums

    def announce_last(sums):
        sums = sums + energy_mine[0]
        energy_mine[0] = sums
        energy_mine[1] = sums * mass_ref[my_slab]

        @pl.loop(1, everyone)
        def _(step):
            energy_copy((flat + step) % everyone, flat).start()

        pltpu.make_async_copy(energy_mine, energy_all.at[flat], local_sems.at[4]).start()

    middle(0, 1, 2, got_a, back_a, home_a, announce_first)

    loads[2].wait()
    loads[3].wait()
    blocks = 3 * LANES // fine_rows

    @pl.loop(0, quarters)
    def _(quarter):
        @pl.loop(0, blocks)
        def _(block):
            at = quarter * blocks + block
            cos_c, sin_c = back_coarse[0, pl.ds(at, 1)], back_coarse[1, pl.ds(at, 1)]
            span = pl.ds(pl.multiple_of(block * fine_rows, fine_rows), fine_rows)
            value_high, value_low = halves(cos_c * back_fine[0] - sin_c * back_fine[1])
            back_table[quarter, 0, span] = value_high
            back_table[quarter, 1, span] = value_low

    out_ref[...] = jnp.zeros_like(out_ref)

    @pl.loop(0, wav)
    def _(w):
        arrive(sent_b, got_b, 1, w)
        rest[w] = unpack(got_b[w, rows:])

    middle(1, 2, 3, got_b, back_b, home_b, announce_last)
    own_energy = pltpu.make_async_copy(energy_mine, energy_all.at[flat], local_sems.at[4])

    def finish(first, count, phase, back, home):
        @pl.loop(0, quarters)
        def _(step):
            quarter = quarter_of((step + quarters - 1) % quarters)
            stacked = []
            for slab in range(slabs):
                w = quarter * slabs + slab
                arrive(back, home, phase, w)
                tiles = [home[w, :rows]]
                if count > 1:
                    tiles.append(unpack(home[w, rows:]))
                stacked.append(jnp.concatenate(tiles, 1) if count > 1 else tiles[0])
            left = halves(jnp.concatenate(stacked, 0))
            span = slice(first * LANES, (first + count) * LANES)
            out_ref[...] += product(left, (back_table[quarter, 0, span], back_table[quarter, 1, span]))

    finish(0, 1, 2, back_a, home_a)
    finish(1, 2, 3, back_b, home_b)
    own_energy.wait()

    @pl.loop(1, everyone)
    def _(step):
        source = (flat + step) % everyone
        energy_copy(source, source).wait()

    total = energy_all[0, 1]
    for n in range(1, everyone):
        total = total + energy_all[n, 1]
    total_ref[0] = jnp.sum(total) / (lev * slabs)
    for slab in range(slabs):
        tile = energy_all[level * wav + slab, 0]
        for quarter in range(1, quarters):
            tile = tile + energy_all[level * wav + quarter * slabs + slab, 0]
        energy_ref[slab] = jnp.sum(tile)


def cos_sin(phases, length):
    angles = 2.0 * np.pi / length * (phases % length)
    return np.stack([np.cos(angles), np.sin(angles)])


def fused(grid_field, truncation_limit, diffusion_order, diffusion_strength, mass_weight):
    slabs, rows, length = grid_field.shape
    wav, lev = lax.axis_size("wav"), lax.axis_size("lev")
    quarters = wav // slabs
    columns = length // 2 // quarters
    tail = columns + 1 - LANES
    groups = LANES // tail
    group_rows = -(-(-(-2 * rows // groups)) // 8) * 8
    padded = -(-rows // 16) * 16
    fine_rows = 32
    sizes = (slabs, rows, length, wav, lev, quarters, columns, padded, tail, groups, group_rows, fine_rows)
    starts = np.arange(quarters) * columns
    place = np.arange(3 * LANES)
    column = place // LANES * HALF + place % HALF
    phase = (place % LANES >= HALF) * (length // 4)
    waves = starts[:, None] + column[None]
    steps = np.arange(length // fine_rows) * fine_rows
    near = np.arange(fine_rows)
    positions = np.arange(length)
    single = lambda array: jnp.asarray(array, jnp.float32)
    coarse = single(cos_sin(steps[None, :, None] * waves[:, None, :], length))
    fine = single(cos_sin(near[None, :, None] * waves[:, None, :] + phase, length))
    back_starts = waves[:, ::fine_rows].reshape(-1)
    back_phase = np.tile(phase[::fine_rows], quarters)
    back_coarse = single(cos_sin(back_starts[:, None] * positions[None] + back_phase[:, None], length))
    back_fine = single(cos_sin(near[:, None] * positions[None], length))
    inner = np.arange(padded)
    turns = cos_sin(np.arange(wav)[:, None, None] * inner[None, :, None], length)
    twiddle = single(np.repeat(turns, HALF, 3).transpose(1, 2, 0, 3).reshape(wav, padded, LANES))
    base_exact = cos_sin(wav * inner[:, None] * inner[None], length)
    base_exact = base_exact * ((inner[:, None] < rows) & (inner[None] < rows))
    base_exact = base_exact.reshape(2 * padded, padded).astype(np.float32)
    base_high = base_exact.astype(jnp.bfloat16)
    base_low = (base_exact - base_high.astype(np.float32)).astype(jnp.bfloat16)
    base = jnp.asarray(np.concatenate([base_high, base_low, base_high], 1))
    limits = truncation_limit.reshape(1, length)
    chunk_a = pltpu.VMEM((wav, rows, LANES), jnp.float32)
    chunk_b = pltpu.VMEM((wav, rows + group_rows, LANES), jnp.float32)
    everyone = wav * lev
    vmem, smem, anywhere = (pl.BlockSpec(memory_space=m) for m in (pltpu.VMEM, pltpu.SMEM, pl.ANY))
    f32, bf16 = jnp.float32, jnp.bfloat16
    filtered, energies, total = pl.pallas_call(
        functools.partial(fused_kernel, sizes),
        out_shape=(
            jax.ShapeDtypeStruct((slabs * rows, length), f32),
            jax.ShapeDtypeStruct((slabs,), f32),
            jax.ShapeDtypeStruct((1,), f32),
        ),
        in_specs=[vmem, vmem, smem, smem, smem, vmem, vmem] + [anywhere] * 4,
        out_specs=(vmem, smem, smem),
        scratch_shapes=[
            pltpu.VMEM((2, slabs * rows, length), bf16),
            pltpu.VMEM((2, length, 2 * LANES), bf16),
            pltpu.VMEM((quarters, 2, 3 * LANES, length), bf16),
            pltpu.VMEM(back_coarse.shape, f32),
            pltpu.VMEM(back_fine.shape, f32),
            pltpu.VMEM(twiddle.shape, f32),
            pltpu.VMEM(base.shape, bf16),
            chunk_a, chunk_a, chunk_b, chunk_b, chunk_a, chunk_a, chunk_b, chunk_b,
            pltpu.VMEM((wav, rows, LANES), f32),
            pltpu.VMEM((wav, padded, 2 * LANES), f32),
            pltpu.VMEM((wav, padded, 3 * LANES), f32),
            pltpu.VMEM((2, 8, LANES), f32),
            pltpu.VMEM((everyone, 2, 8, LANES), f32),
            pltpu.SemaphoreType.DMA((4,)),
            pltpu.SemaphoreType.DMA((4, wav)),
            pltpu.SemaphoreType.DMA((4, wav)),
            pltpu.SemaphoreType.DMA((everyone,)),
            pltpu.SemaphoreType.DMA((everyone,)),
            pltpu.SemaphoreType.DMA((5,)),
        ],
        compiler_params=pltpu.CompilerParams(
            collective_id=0, has_side_effects=True, vmem_limit_bytes=60 * 1024 * 1024
        ),
        name="fused_step",
    )(
        grid_field.reshape(slabs * rows, length), limits, diffusion_order, diffusion_strength, mass_weight,
        coarse, fine, back_coarse, back_fine, twiddle, base,
    )
    return filtered.reshape(slabs, rows, length), energies, total[0]


def fits(shape):
    slabs, rows, length = shape
    wav = lax.axis_size("wav")
    if wav != 8 or slabs != 2 or rows % 8 or length % 16 or length != rows * wav:
        return False
    columns = length * slabs // 2 // wav
    return length % 32 == 0 and LANES <= columns < LANES + LANES // 2


def local(grid_field, truncation_limit, diffusion_order, diffusion_strength, mass_weight):
    slab_count, row_count, length = grid_field.shape
    if fits(grid_field.shape):
        return fused(
            grid_field, truncation_limit, diffusion_order, diffusion_strength, mass_weight
        )
    cosine_table, sine_table = tables(length)
    filtered, partial_value = half_plane(
        grid_field, truncation_limit, diffusion_order, diffusion_strength, cosine_table, sine_table
    )
    total_slabs = lax.axis_size("lev") * slab_count
    energies = lax.psum(partial_value, "wav")
    weighted_sum = lax.psum(jnp.sum(mass_weight * energies), "lev")
    total_energy = weighted_sum / total_slabs
    return (filtered, energies, total_energy)


def solution(mesh):
    placed = (P("lev", "wav", None), P(), P("lev"), P("lev"), P("lev"))
    return jax.shard_map(
        local,
        mesh=mesh,
        in_specs=placed,
        out_specs=(P("lev", "wav", None), P("lev"), P()),
        check_vma=False,
    )
```

profile of v0, /device:TPU:1, one launch (start us, length us, event | category | flops | bytes accessed | tf_op | source)
XLA Modules:
  0.0 56.7 jit_solution(2404103383467118767)
XLA Ops:
  0.6 1.3 %reshape.16.limit_ref = s32[1,1216]{1,0:T(1,128)} reshape(s32[1216]{0:T(1024)} %param.12) | data formatting | bytes 9728 | tf_op jit(solution)/shard_map/reshape | solution.py:542
  1.9 49.9 %fused_step.1 = (f32[304,1216]{1,0:T(8,128)}, f32[2]{0:T(128)}, f32[1]{0:T(128)}) custom-call(f32[304,1216]{1,0:T(8,128)} %bitcast.3, s32[1,1216]{1,0:T(1,128)} %reshape.16.limit_ref, s32[2]{0:T(128)} %order_ref.1, f32[2]{0:T(128)} %strength_ref.1, f32[2]{0:T(128)} %mass_ref.1, f32[2,4,38,384]{3,2,1,0:T(8,128)} %constant.12.clone.coarse_ref, ...), custom_call_target="tpu_custom_call" | custom-call | tf_op jit(solution)/shard_map/fused_step/pallas_call | solution.py:548
  51.8 0.0 copy-start
  51.8 2.6 %copy.17 = f32[2,152,1216]{2,1,0:T(8,128)} copy(f32[2,152,1216]{2,1,0:T(8,128)} %bitcast.4) | data formatting | bytes 2957312
  54.5 0.0 copy-done
  54.5 0.5 copy.18
Async XLA Ops:
  51.8 2.7 %copy-start = (f32[2]{0:T(128)S(1)}, f32[2]{0:T(128)}, u32[]{:S(2)}) copy-start(f32[2]{0:T(128)} %get-tuple-element.13) | copy-start | bytes 28
where the time goes:
time: 57 us; the launch traced here: 56.7 us
  Pallas kernels  49.9 us (88%)
  local copies, waits for them, and re-layouts  4.45 us (8%)
  between operations  2.41 us (4%)
    pallas_call x1, Pallas kernels, fused(): pl.pallas_call(functools.partial(fused_kernel, sizes), out_shape=(jax.Sha...  49.9 us
    unnamed x4, local copies, waits for them, and re-layouts  3.16 us
    reshape x1, local copies, waits for them, and re-layouts, fused(): limits = truncation_limit.reshape(1, length)  1.29 us

commit v1 on v0

v1 whole, which is shorter than its diff:
```python
import functools

import jax
import jax.numpy as jnp
import numpy as np
from jax import lax
from jax.experimental import pallas as pl
from jax.experimental.pallas import tpu as pltpu
from jax.sharding import PartitionSpec as P

product_precision = lax.Precision.HIGH


def tables(length):
    step = 32
    coarse = -(-length // step)
    columns = np.arange(length)
    high = 2.0 * np.pi / length * (np.arange(coarse)[:, None] * step * columns[None, :] % length)
    low = 2.0 * np.pi / length * (np.arange(step)[:, None] * columns[None, :] % length)
    cos_high, sin_high = (jnp.asarray(f(high), jnp.float32)[:, None] for f in (np.cos, np.sin))
    cos_low, sin_low = (jnp.asarray(f(low), jnp.float32)[None] for f in (np.cos, np.sin))
    cosine = cos_high * cos_low - sin_high * sin_low
    sine = sin_high * cos_low + cos_high * sin_low
    return tuple(t.reshape(coarse * step, length)[:length] for t in (cosine, sine))


def signed(positions, length):
    return jnp.where(positions < length // 2, positions, positions - length)


def transform(values, cosine_table, sine_table, direction):
    with_cosine = jnp.einsum("scpi,iq->scpq", values, cosine_table, precision=product_precision)
    with_sine = jnp.einsum("scpi,iq->scpq", values, sine_table, precision=product_precision)
    if direction < 0:
        real_part = with_cosine[:, 0] + with_sine[:, 1]
        imaginary = with_cosine[:, 1] - with_sine[:, 0]
    else:
        real_part = with_cosine[:, 0] - with_sine[:, 1]
        imaginary = with_cosine[:, 1] + with_sine[:, 0]
    return jnp.stack([real_part, imaginary], axis=1)


def damping(wave_rows, limits, length, diffusion_order, diffusion_strength):
    wave_first = signed(jnp.arange(length, dtype=jnp.int32), length)
    rows_float = wave_rows.astype(jnp.float32)
    first_float = wave_first.astype(jnp.float32)
    scaled_radius = (rows_float[:, None] ** 2 + first_float[None, :] ** 2) / (0.5 * length) ** 2
    inside = (jnp.abs(wave_first)[None, :] <= limits[:, None]).astype(jnp.float32)
    powered = jnp.power(scaled_radius[None], diffusion_order.astype(jnp.float32)[:, None, None])
    return inside[None] / (1.0 + diffusion_strength[:, None, None] * powered)


def mirrored(values):
    return jnp.roll(jnp.flip(values, -1), 1, -1)


def half_plane(
    grid_field, truncation_limit, diffusion_order, diffusion_strength, cosine_table, sine_table
):
    length = grid_field.shape[2]
    half = length // 2
    row_real = jnp.einsum("sij,jl->sli", grid_field, cosine_table[:, :half], precision=product_precision)
    row_imag = -jnp.einsum("sij,jl->sli", grid_field, sine_table[:, :half], precision=product_precision)
    nyquist = jnp.einsum("sij,j->si", grid_field, cosine_table[:, half], precision=product_precision)
    zero_row = (jnp.arange(half, dtype=jnp.int32) == 0)[None, :, None]
    row_imag = jnp.where(zero_row, nyquist[:, None, :], row_imag)
    along_rows = jnp.stack([row_real, row_imag], axis=1)
    spectrum = transform(
        lax.all_to_all(along_rows, "wav", split_axis=2, concat_axis=3, tiled=True),
        cosine_table,
        sine_table,
        -1,
    )
    column_count = spectrum.shape[2]
    wav_index = lax.axis_index("wav")
    offset = wav_index * column_count
    wave_rows = offset + jnp.arange(column_count, dtype=jnp.int32)
    limits = lax.dynamic_slice(truncation_limit, (offset,), (column_count,))
    damp_main = damping(wave_rows, limits, length, diffusion_order, diffusion_strength)
    nyquist_rows = signed(jnp.full((1,), half, jnp.int32), length)
    damp_top = damping(
        nyquist_rows, truncation_limit[half : half + 1], length, diffusion_order, diffusion_strength
    )[:, 0]
    damped = spectrum * damp_main[:, None]
    packed_real = spectrum[:, 0, 0, :]
    packed_imag = spectrum[:, 1, 0, :]
    back_real = mirrored(packed_real)
    back_imag = mirrored(packed_imag)
    zero_real = (packed_real + back_real) * 0.5 * damp_main[:, 0]
    zero_imag = (packed_imag - back_imag) * 0.5 * damp_main[:, 0]
    top_real = (packed_imag + back_imag) * 0.5 * damp_top
    top_imag = (back_real - packed_real) * 0.5 * damp_top
    is_zero = wave_rows == 0
    column_weight = jnp.where(is_zero, 0.0, 2.0).astype(jnp.float32)
    edge = jnp.sum(zero_real**2 + zero_imag**2 + top_real**2 + top_imag**2, axis=-1)
    main_sum = jnp.sum(damped * damped * column_weight[None, None, :, None], axis=(1, 2, 3))
    partial_value = (main_sum + jnp.where(wav_index == 0, edge, 0.0)) / float(length) ** 4
    zero_column = is_zero[None, :, None]
    repacked = jnp.stack(
        [
            jnp.where(zero_column, (zero_real - top_imag)[:, None, :], damped[:, 0]),
            jnp.where(zero_column, (zero_imag + top_real)[:, None, :], damped[:, 1]),
        ],
        axis=1,
    )
    along_first = transform(repacked, cosine_table, sine_table, 1)
    inverse_area = 1.0 / float(length) ** 2
    received = lax.all_to_all(along_first, "wav", split_axis=3, concat_axis=2, tiled=True)
    row_weight = jnp.where(jnp.arange(half, dtype=jnp.int32) == 0, 1.0, 2.0).astype(jnp.float32)[
        :, None
    ]
    with_cosine = jnp.einsum(
        "spi,pj->sij", received[:, 0] * row_weight, cosine_table[:half], precision=product_precision
    )
    with_sine = jnp.einsum(
        "spi,pj->sij", received[:, 1] * row_weight, sine_table[:half], precision=product_precision
    )
    top_term = received[:, 1, 0, :][:, :, None] * cosine_table[half][None, None, :]
    filtered = (with_cosine - with_sine + top_term) * inverse_area
    return (filtered, partial_value)


LANES = 128
HALF = LANES // 2
MESH = pl.DeviceIdType.MESH


def halves(values):
    high = values.astype(jnp.bfloat16)
    return high, (values - high.astype(jnp.float32)).astype(jnp.bfloat16)


def product(left, right):
    dot = functools.partial(jnp.dot, preferred_element_type=jnp.float32)
    return dot(left[0], right[0]) + dot(left[1], right[0]) + dot(left[0], right[1])


def swap(value):
    count = value.shape[1] // LANES
    turned = [pltpu.roll(value[:, n * LANES : (n + 1) * LANES], HALF, 1) for n in range(count)]
    return jnp.concatenate(turned, 1) if count > 1 else turned[0]


def eight_points(x, sign, signs):
    turn = signs if sign < 0 else -signs

    def four(p, q, r, t):
        a0, a1, a2, a3 = p + r, p - r, q + t, swap(q - t) * turn
        return a0 + a2, a1 + a3, a0 - a2, a1 - a3

    e = four(x[0], x[2], x[4], x[6])
    o = four(x[1], x[3], x[5], x[7])
    root = 0.5**0.5
    odd = (
        o[0],
        root * (o[1] + swap(o[1]) * turn),
        swap(o[2]) * turn,
        root * (swap(o[3]) * turn - o[3]),
    )
    return [e[n] + odd[n] for n in range(4)] + [e[n] - odd[n] for n in range(4)]


def pieces(rows, group_rows, groups):
    found = []
    for group in range(groups):
        start, stop = group * group_rows, min((group + 1) * group_rows, 2 * rows)
        while start < stop:
            part = start // rows
            end = min(stop, (part + 1) * rows)
            found.append((group, start - group * group_rows, part, start - part * rows, end - start))
            start = end
    return found


def fused_kernel(
    sizes,
    grid_hbm, limit_hbm, order_hbm, strength_hbm, mass_hbm, coarse_hbm, fine_hbm,
    back_coarse_hbm, back_fine_hbm, twiddle_hbm, base_hbm,
    sum_ref, tail_ref, tail_table, energy_ref,
    grid, limit_ref, order_ref, strength_ref, mass_ref, coarse_ref, fine_ref,
    back_coarse, back_fine, twiddle, base, grid_parts, table, back_table,
    sent_a, sent_b, sent_c, got_a, got_b, got_c, back_a, back_b, back_c, home_a, home_b, home_c,
    rest, work, damp, energy_sums, energy_mine, energy_wav, energy_lev,
    load_sems, send_sems, recv_sems, local_sems, wav_send, wav_recv, lev_send, lev_recv, ready,
):
    slabs, rows, length, wav, lev, quarters, columns, padded, tail, groups, group_rows, fine_rows = sizes
    half = length // 2
    quarter_lanes = LANES // 2
    part_lanes = quarter_lanes // 2
    me = lax.axis_index("wav")
    level = lax.axis_index("lev")
    my_quarter, my_slab = me // slabs, me % slabs

    barrier = pltpu.get_barrier_semaphore()

    @pl.loop(1, wav)
    def _(step):
        pl.semaphore_signal(barrier, inc=1, device_id=(level, (me + step) % wav), device_id_type=MESH)

    for other in range(1, lev):
        @pl.when(level < other)
        def _():
            pl.semaphore_signal(barrier, inc=1, device_id=(other, me), device_id_type=MESH)

    loads = [
        pltpu.make_async_copy(src, dst, load_sems.at[n])
        for n, (src, dst) in enumerate(
            (
                (coarse_hbm, coarse_ref), (fine_hbm, fine_ref), (grid_hbm, grid),
                (limit_hbm, limit_ref), (order_hbm, order_ref), (strength_hbm, strength_ref),
                (mass_hbm, mass_ref), (twiddle_hbm, twiddle), (base_hbm, base),
                (back_coarse_hbm, back_coarse), (back_fine_hbm, back_fine),
            )
        )
    ]
    for load in loads:
        load.start()

    def quarter_of(step):
        down, across = 1 - step % 2, 1 - step // 2
        y, x = my_quarter // 2, my_quarter % 2
        return (y + down - 2 * y * down) * 2 + (x + across - 2 * x * across)

    def push(source, target, phase, w):
        @pl.when(w != me)
        def _():
            pltpu.make_async_remote_copy(
                src_ref=source.at[w], dst_ref=target.at[me],
                send_sem=send_sems.at[phase, w], recv_sem=recv_sems.at[phase, me],
                device_id=(level, w), device_id_type=MESH,
            ).start()

        @pl.when(w == me)
        def _():
            pltpu.make_async_copy(source.at[w], target.at[w], local_sems.at[phase]).start()

    def push_all(source, target, phase):
        @pl.loop(0, quarters)
        def _(step):
            for slab in range(slabs):
                push(source, target, phase, quarter_of(step) * slabs + slab)

    def arrive(source, target, phase, w):
        @pl.when(w != me)
        def _():
            pltpu.make_async_remote_copy(
                src_ref=source.at[w], dst_ref=target.at[w],
                send_sem=send_sems.at[phase, w], recv_sem=recv_sems.at[phase, w],
                device_id=(level, w), device_id_type=MESH,
            ).wait()

        @pl.when(w == me)
        def _():
            pltpu.make_async_copy(source.at[w], target.at[w], local_sems.at[phase]).wait()

    lane = lax.broadcasted_iota(jnp.int32, (1, LANES), 1)
    signs = jnp.where(lane < HALF, 1.0, -1.0)
    layout = pieces(rows, group_rows, groups)
    wide = (0, HALF)

    def inside_part(starts, part):
        return (lane >= starts[part]) & (lane < starts[part] + tail)

    def pack(tile, starts):
        shifted = {}
        for group, at, part, start, count in layout:
            piece = jnp.where(inside_part(starts, part), tile(start, count), 0.0)
            shift = (group * tail - starts[part]) % LANES
            shifted.setdefault(group, []).append(pltpu.roll(piece, shift, 1) if shift else piece)
        packed = jnp.zeros((group_rows, LANES), jnp.float32)
        for found in shifted.values():
            whole = jnp.concatenate(found, 0) if len(found) > 1 else found[0]
            if whole.shape[0] < group_rows:
                fill = jnp.zeros((group_rows - whole.shape[0], LANES), jnp.float32)
                whole = jnp.concatenate([whole, fill], 0)
            packed = packed + whole
        return packed

    def unpack(packed, starts):
        found = {0: [], 1: []}
        for group, at, part, start, count in layout:
            piece = packed[at : at + count]
            shift = (starts[part] - group * tail) % LANES
            piece = pltpu.roll(piece, shift, 1) if shift else piece
            found[part].append(jnp.where(inside_part(starts, part), piece, 0.0))
        return jnp.concatenate(found[0], 0) + jnp.concatenate(found[1], 0)

    def quarter_starts(quarter):
        first = quarter % 2 * quarter_lanes
        return (first, first + part_lanes)

    loads[0].wait()
    loads[1].wait()

    @pl.loop(0, quarters + 1)
    def _(step):
        last = step // quarters
        piece = quarter_of(step % quarters) * (1 - last) + quarters * last
        cos_f, sin_f = fine_ref[0, piece], fine_ref[1, piece]

        @pl.loop(0, length // fine_rows, unroll=2)
        def _(block):
            cos_c, sin_c = coarse_ref[0, piece, pl.ds(block, 1)], coarse_ref[1, piece, pl.ds(block, 1)]
            span = pl.ds(pl.multiple_of(block * fine_rows, fine_rows), fine_rows)
            value_high, value_low = halves(cos_c * cos_f - sin_c * sin_f)
            table[0, span] = value_high
            table[1, span] = value_low

        @pl.when(step == 0)
        def _():
            loads[2].wait()
            high, low = halves(grid[...])
            grid_parts[0] = high
            grid_parts[1] = low

        result = product((grid_parts[0], grid_parts[1]), (table[0], table[1]))
        for slab in range(slabs):
            w = piece * slabs + slab
            sent_a[w] = result[slab * rows : (slab + 1) * rows, :LANES]
            sent_b[w] = result[slab * rows : (slab + 1) * rows, LANES:]

        @pl.when(step == 0)
        def _():
            pl.semaphore_wait(barrier, wav - 1 + level)

        @pl.when(step < quarters)
        def _():
            for slab in range(slabs):
                push(sent_a, got_a, 0, piece * slabs + slab)

        @pl.when(step == quarters - 1)
        def _():
            push_all(sent_b, got_b, 1)

    for quarter in range(quarters):
        from_ref = sent_b if quarter // 2 else sent_a
        for slab in range(slabs):
            sent_c[quarter * slabs + slab] = pack(
                lambda start, many: from_ref[wav + slab, start : start + many], quarter_starts(quarter)
            )
    push_all(sent_c, got_c, 2)

    for other in range(lev - 1):
        @pl.when(other < level)
        def _():
            pl.semaphore_signal(ready.at[level], inc=1, device_id=(other, me), device_id_type=MESH)

    for load in loads[3:]:
        load.wait()
    place = lax.broadcasted_iota(jnp.int32, (1, 3 * LANES), 1)
    column = place // LANES * HALF + place % HALF
    wave = my_quarter * columns + column
    valid = (column < columns) | ((column == columns) & (wave == half))
    single = (wave == 0) | (wave == half)
    out_weight = jnp.where(single, 1.0, 2.0) / float(length) ** 2
    energy_weight = jnp.where(single, 1.0, 0.5)
    all_limits = limit_ref[...].reshape(1, length)
    limits = jnp.full((1, 3 * LANES), -1, jnp.int32)
    for quarter in range(quarters):
        found = []
        for tile in range(3):
            start = quarter * columns + tile * HALF
            found += [all_limits[:, start : start + HALF]] * 2
        limits = jnp.where(my_quarter == quarter, jnp.concatenate(found, 1), limits)
    limits = jnp.where(valid, limits, -1)
    order = order_ref[my_slab]
    strength = strength_ref[my_slab]
    wave_square = wave.astype(jnp.float32) ** 2

    @pl.loop(0, wav)
    def _(m):
        row = lax.broadcasted_iota(jnp.int32, (padded, 1), 0)
        q = row * wav + m
        signed_q = jnp.where(q < half, q, q - length)
        radius = (wave_square + signed_q.astype(jnp.float32) ** 2) / (0.5 * length) ** 2
        square = radius * radius
        powered = jnp.where(order >= 3, square, 1.0) * jnp.where(order % 2 == 1, radius, square)
        inside = (jnp.abs(signed_q) <= limits) & (row < rows)
        damp[m] = jnp.where(inside, out_weight / (1.0 + strength * powered), 0.0)
        work[m, rows:] = jnp.zeros((padded - rows, LANES), jnp.float32)

    blocks = LANES // fine_rows
    plain = 2 * quarters * blocks

    def back_piece(at, target, span):
        cos_c, sin_c = back_coarse[0, pl.ds(at, 1)], back_coarse[1, pl.ds(at, 1)]
        value_high, value_low = halves(cos_c * back_fine[0] - sin_c * back_fine[1])
        target[0, span] = value_high
        target[1, span] = value_low

    @pl.loop(0, 2 * quarters)
    def _(n):
        @pl.loop(0, blocks)
        def _(block):
            span = pl.ds(pl.multiple_of(block * fine_rows, fine_rows), fine_rows)
            back_piece(n * blocks + block, back_table.at[n], span)

    @pl.loop(0, 2 * blocks)
    def _(block):
        back_piece(plain + block, tail_table, pl.ds(pl.multiple_of(block * fine_rows, fine_rows), fine_rows))

    sum_ref[...] = jnp.zeros_like(sum_ref)
    energy_sums[...] = jnp.zeros_like(energy_sums)

    def along(value):
        value_high, value_low = halves(value)
        stacked = jnp.concatenate([value_high, value_high, value_low], 0)
        return jnp.dot(base[...], stacked, preferred_element_type=jnp.float32)

    block_rows = 24
    batch = 2

    def in_blocks(body):
        @pl.loop(0, rows // block_rows)
        def _(block):
            body(pl.multiple_of(block * block_rows, 8), block_rows)

        if rows % block_rows:
            body(rows - rows % block_rows, rows % block_rows)

    def middle(tile, source, target):
        span_of = slice(tile * LANES, (tile + 1) * LANES)
        all_signs = jnp.concatenate([signs] * batch, 1)

        def split(start, many):
            span = pl.ds(start, many)
            for m, value in enumerate(eight_points([source[w, span] for w in range(wav)], -1, signs)):
                work[m, span] = value

        in_blocks(split)

        def residues(first, sums):
            found = range(first, first + batch)
            beside = lambda pick: jnp.concatenate([pick(m) for m in found], 1)
            packed_turn = beside(lambda m: twiddle[m])
            other_turn = swap(packed_turn)
            low = jnp.concatenate([lane] * batch, 1) < HALF
            cos_t = jnp.where(low, packed_turn, other_turn)
            sin_t = jnp.where(low, other_turn, -packed_turn)
            value = beside(lambda m: work[m])
            both = along(value * cos_t + swap(value) * sin_t)
            value = both[:padded] + swap(both[padded:]) * all_signs
            value = value * beside(lambda m: damp[m, :, span_of])
            sums = sums + jnp.sum((value * value).reshape(padded // 8, 8, batch * LANES), axis=0)
            both = along(value)
            value = both[:padded] - swap(both[padded:]) * all_signs
            value = value * cos_t - swap(value) * sin_t
            for n, m in enumerate(found):
                work[m] = value[:, n * LANES : (n + 1) * LANES]
            return sums

        sums = jnp.zeros((8, batch * LANES), jnp.float32)
        for first in range(0, wav, batch):
            sums = residues(first, sums)
        sums = sum(sums[:, n * LANES : (n + 1) * LANES] for n in range(batch))
        energy_sums[...] += sums * energy_weight[:, span_of]

        if tile == 2:
            announce()

        def join(start, many):
            span = pl.ds(start, many)
            for w, value in enumerate(eight_points([work[m, span] for m in range(wav)], 1, signs)):
                target[w, span] = value

        in_blocks(join)

    def wav_copy(target, slot):
        return pltpu.make_async_remote_copy(
            src_ref=energy_mine, dst_ref=energy_wav.at[slot],
            send_sem=wav_send.at[target], recv_sem=wav_recv.at[slot],
            device_id=(level, target), device_id_type=MESH,
        )

    def lev_copy(target, slot):
        return pltpu.make_async_remote_copy(
            src_ref=energy_lev.at[level], dst_ref=energy_lev.at[slot],
            send_sem=lev_send.at[target], recv_sem=lev_recv.at[slot],
            device_id=(target, me), device_id_type=MESH,
        )

    def announce():
        mine = jnp.sum(energy_sums[...], axis=0, keepdims=True)
        energy_mine[...] = mine
        energy_wav[me] = mine

        @pl.loop(1, wav)
        def _(step):
            wav_copy((me + step) % wav, me).start()

    @pl.loop(0, wav)
    def _(w):
        arrive(sent_a, got_a, 0, w)

    middle(0, got_a, back_a)
    push_all(back_a, home_a, 3)

    @pl.loop(0, wav)
    def _(w):
        arrive(sent_b, got_b, 1, w)

    middle(1, got_b, back_b)
    push_all(back_b, home_b, 4)

    @pl.loop(0, wav)
    def _(w):
        arrive(sent_c, got_c, 2, w)
        rest[w] = unpack(got_c[w], wide)

    middle(2, rest, rest)

    @pl.loop(0, quarters)
    def _(step):
        for slab in range(slabs):
            w = quarter_of(step) * slabs + slab
            back_c[w] = pack(lambda start, many: rest[w, start : start + many], wide)
            push(back_c, home_c, 5, w)

    def finish(tile, phase, back, home):
        @pl.loop(0, quarters // 2)
        def _(pair):
            found, right = [], ([], [])
            for n in range(2):
                quarter = quarter_of((2 * pair + n + quarters - 1) % quarters)
                stacked = []
                for slab in range(slabs):
                    w = quarter * slabs + slab
                    arrive(back, home, phase, w)
                    stacked.append(home[w])
                found.append(jnp.concatenate(stacked, 0))
                for part in range(2):
                    right[part].append(back_table[tile * quarters + quarter, part])
            left = halves(jnp.concatenate(found, 1))
            sum_ref[...] += product(left, [jnp.concatenate(part, 0) for part in right])

    finish(0, 3, back_a, home_a)
    finish(1, 4, back_b, home_b)

    @pl.loop(1, wav)
    def _(step):
        source = (me + step) % wav
        wav_copy(source, source).wait()

    slab_sums = []
    for slab in range(slabs):
        total = energy_wav[slab]
        for quarter in range(1, quarters):
            total = total + energy_wav[quarter * slabs + slab]
        slab_sums.append(total)
    weighted = slab_sums[0] * mass_ref[0]
    for slab in range(1, slabs):
        weighted = weighted + slab_sums[slab] * mass_ref[slab]
    energy_lev[level] = weighted

    for other in range(1, lev):
        @pl.when(level < other)
        def _():
            pl.semaphore_wait(ready.at[other], 1)

    for other in range(lev):
        @pl.when(level != other)
        def _():
            lev_copy(other, level).start()

    @pl.loop(0, wav)
    def _(w):
        arrive(back_c, home_c, 5, w)

    for side in range(2):
        for slab in range(slabs):
            value = sum(
                unpack(home_c[quarter * slabs + slab], quarter_starts(quarter))
                for quarter in range(2 * side, 2 * side + 2)
            )
            value_high, value_low = halves(value)
            at = (slice(slab * rows, (slab + 1) * rows), slice(side * LANES, (side + 1) * LANES))
            tail_ref[(0,) + at] = value_high
            tail_ref[(1,) + at] = value_low

    for other in range(lev):
        @pl.when(level != other)
        def _():
            lev_copy(other, other).wait()

    total = energy_lev[0]
    for other in range(1, lev):
        total = total + energy_lev[other]
    fill = jnp.zeros((8 - slabs - 1, LANES), jnp.float32)
    energy_ref[...] = jnp.concatenate(slab_sums + [total / (lev * slabs), fill], 0)


def last_kernel(
    slabs, spans, sum_ref, tail_ref, tail_table, energy_ref, out_hbm, energies_hbm, total_hbm,
    out, energies, total, sems,
):
    sums = jnp.sum(energy_ref[...], axis=1, keepdims=True)
    for slab in range(slabs):
        energies[slab] = sums[slab, 0]
    total[0] = sums[slabs, 0]
    copies = [
        pltpu.make_async_copy(energies, energies_hbm, sems.at[0]),
        pltpu.make_async_copy(total, total_hbm, sems.at[1]),
    ]
    for copy in copies:
        copy.start()
    left = (tail_ref[0], tail_ref[1])
    for n, (start, stop) in enumerate(spans):
        out[:, start:stop] = sum_ref[:, start:stop] + product(
            left, (tail_table[0, :, start:stop], tail_table[1, :, start:stop])
        )
        copies.append(
            pltpu.make_async_copy(out.at[:, start:stop], out_hbm.at[:, start:stop], sems.at[2 + n])
        )
        copies[-1].start()
    for copy in copies:
        copy.wait()


def cos_sin(phases, length):
    angles = 2.0 * np.pi / length * (phases % length)
    return np.stack([np.cos(angles), np.sin(angles)])


def fused(grid_field, truncation_limit, diffusion_order, diffusion_strength, mass_weight):
    slabs, rows, length = grid_field.shape
    wav, lev = lax.axis_size("wav"), lax.axis_size("lev")
    quarters = wav // slabs
    columns = length // 2 // quarters
    tail = columns + 1 - LANES
    groups = LANES // tail
    group_rows = -(-(-(-2 * rows // groups)) // 8) * 8
    padded = -(-rows // 16) * 16
    fine_rows = 32
    sizes = (slabs, rows, length, wav, lev, quarters, columns, padded, tail, groups, group_rows, fine_rows)
    turn = length // 4
    place = np.arange(2 * LANES)
    starts = np.arange(quarters) * columns
    plain_waves = starts[:, None] + (place // LANES * HALF + place % HALF)[None]
    plain_phase = np.broadcast_to((place % LANES >= HALF) * turn, plain_waves.shape)
    part = LANES // 4
    tail_waves = (starts[place // HALF] + LANES + place % part)[None]
    tail_phase = (place % HALF >= part)[None] * turn
    waves = np.concatenate([plain_waves, tail_waves])
    phase = np.concatenate([plain_phase, tail_phase])
    steps = np.arange(length // fine_rows) * fine_rows
    near = np.arange(fine_rows)
    positions = np.arange(length)
    single = lambda array: jnp.asarray(array, jnp.float32)
    coarse = single(cos_sin(steps[None, :, None] * waves[:, None, :], length))
    fine = single(cos_sin(near[None, :, None] * waves[:, None, :] + phase[:, None, :], length))
    by_tile = lambda array: np.concatenate(
        [array[:quarters, :LANES].ravel(), array[:quarters, LANES:].ravel(), array[quarters]]
    )[::fine_rows]
    back_coarse = single(
        cos_sin(by_tile(waves)[:, None] * positions[None] + by_tile(phase)[:, None], length)
    )
    back_fine = single(cos_sin(near[:, None] * positions[None], length))
    inner = np.arange(padded)
    turns = cos_sin(np.arange(wav)[:, None, None] * inner[None, :, None], length)
    twiddle = single(np.repeat(turns, HALF, 3).transpose(1, 2, 0, 3).reshape(wav, padded, LANES))
    base_exact = cos_sin(wav * inner[:, None] * inner[None], length)
    base_exact = base_exact * ((inner[:, None] < rows) & (inner[None] < rows))
    base_exact = base_exact.reshape(2 * padded, padded).astype(np.float32)
    base_high = base_exact.astype(jnp.bfloat16)
    base_low = (base_exact - base_high.astype(np.float32)).astype(jnp.bfloat16)
    base = jnp.asarray(np.concatenate([base_high, base_low, base_high], 1))
    vmem, hbm = pl.BlockSpec(memory_space=pltpu.VMEM), pl.BlockSpec(memory_space=pltpu.HBM)
    f32, bf16, i32 = jnp.float32, jnp.bfloat16, jnp.int32
    sent = pltpu.VMEM((wav + slabs, rows, LANES), f32)
    whole = pltpu.VMEM((wav, rows, LANES), f32)
    small = pltpu.VMEM((wav, group_rows, LANES), f32)
    dma = pltpu.SemaphoreType.DMA
    partial_sum, tails, tail_table, energy_rows = pl.pallas_call(
        functools.partial(fused_kernel, sizes),
        out_shape=(
            jax.ShapeDtypeStruct((slabs * rows, length), f32),
            jax.ShapeDtypeStruct((2, slabs * rows, 2 * LANES), bf16),
            jax.ShapeDtypeStruct((2, 2 * LANES, length), bf16),
            jax.ShapeDtypeStruct((8, LANES), f32),
        ),
        in_specs=[hbm] * 11,
        out_specs=(vmem,) * 4,
        scratch_shapes=[
            pltpu.VMEM((slabs * rows, length), f32),
            pltpu.VMEM((length,), i32),
            pltpu.SMEM((slabs,), i32),
            pltpu.SMEM((slabs,), f32),
            pltpu.SMEM((slabs,), f32),
            pltpu.VMEM(coarse.shape, f32),
            pltpu.VMEM(fine.shape, f32),
            pltpu.VMEM(back_coarse.shape, f32),
            pltpu.VMEM(back_fine.shape, f32),
            pltpu.VMEM(twiddle.shape, f32),
            pltpu.VMEM(base.shape, bf16),
            pltpu.VMEM((2, slabs * rows, length), bf16),
            pltpu.VMEM((2, length, 2 * LANES), bf16),
            pltpu.VMEM((2 * quarters, 2, LANES, length), bf16),
            sent, sent, small, whole, whole, small, whole, whole, small, whole, whole, small,
            whole,
            pltpu.VMEM((wav, padded, LANES), f32),
            pltpu.VMEM((wav, padded, 3 * LANES), f32),
            pltpu.VMEM((8, LANES), f32),
            pltpu.VMEM((1, LANES), f32),
            pltpu.VMEM((wav, 1, LANES), f32),
            pltpu.VMEM((lev, 1, LANES), f32),
            dma((11,)), dma((6, wav)), dma((6, wav)), dma((6,)),
            dma((wav,)), dma((wav,)), dma((lev,)), dma((lev,)),
            pltpu.SemaphoreType.REGULAR((lev,)),
        ],
        compiler_params=pltpu.CompilerParams(
            collective_id=0, has_side_effects=True, vmem_limit_bytes=40 * 1024 * 1024
        ),
        name="fused_step",
    )(
        *(
            pltpu.with_memory_space_constraint(array, pltpu.HBM)
            for array in (
                grid_field.reshape(slabs * rows, length), truncation_limit, diffusion_order,
                diffusion_strength, mass_weight, coarse, fine, back_coarse, back_fine, twiddle, base,
            )
        )
    )
    spans = [(at, min(at + 2 * LANES, length)) for at in range(0, length, 2 * LANES)]
    filtered, energies, total = pl.pallas_call(
        functools.partial(last_kernel, slabs, spans),
        out_shape=(
            jax.ShapeDtypeStruct((slabs * rows, length), f32),
            jax.ShapeDtypeStruct((slabs,), f32),
            jax.ShapeDtypeStruct((1,), f32),
        ),
        in_specs=[vmem] * 4,
        out_specs=(hbm,) * 3,
        scratch_shapes=[
            pltpu.VMEM((slabs * rows, length), f32),
            pltpu.SMEM((slabs,), f32),
            pltpu.SMEM((1,), f32),
            dma((2 + len(spans),)),
        ],
        compiler_params=pltpu.CompilerParams(vmem_limit_bytes=12 * 1024 * 1024),
        name="last_product",
    )(partial_sum, tails, tail_table, energy_rows)
    return filtered.reshape(slabs, rows, length), energies, total[0]


def fits(shape):
    slabs, rows, length = shape
    wav = lax.axis_size("wav")
    if wav != 8 or slabs != 2 or rows % 8 or length % 16 or length != rows * wav:
        return False
    columns = length * slabs // 2 // wav
    return length % 32 == 0 and LANES <= columns < LANES + LANES // 4


def local(grid_field, truncation_limit, diffusion_order, diffusion_strength, mass_weight):
    slab_count, row_count, length = grid_field.shape
    if fits(grid_field.shape):
        return fused(
            grid_field, truncation_limit, diffusion_order, diffusion_strength, mass_weight
        )
    cosine_table, sine_table = tables(length)
    filtered, partial_value = half_plane(
        grid_field, truncation_limit, diffusion_order, diffusion_strength, cosine_table, sine_table
    )
    total_slabs = lax.axis_size("lev") * slab_count
    energies = lax.psum(partial_value, "wav")
    weighted_sum = lax.psum(jnp.sum(mass_weight * energies), "lev")
    total_energy = weighted_sum / total_slabs
    return (filtered, energies, total_energy)


def solution(mesh):
    placed = (P("lev", "wav", None), P(), P("lev"), P("lev"), P("lev"))
    return jax.shard_map(
        local,
        mesh=mesh,
        in_specs=placed,
        out_specs=(P("lev", "wav", None), P("lev"), P()),
        check_vma=False,
    )
```

time: 57 us -> 46.7 us (0.82)
  Pallas kernels: 49.9 us -> 45.4 us
  local copies, waits for them, and re-layouts: 4.45 us -> 0 us
  between operations: 2.41 us -> 0.64 us
    pallas_call x1, Pallas kernels: 49.9 us -> 43.7 us  [fused(): pl.pallas_call(functools.partial(fused_kernel, sizes), out_shape=(jax.Sha...]
    unnamed x4 -> x0, local copies, waits for them, and re-layouts: 3.16 us -> none
    pallas_call x0 -> x1, Pallas kernels: none -> 1.71 us  [fused(): pl.pallas_call(functools.partial(last_kernel, slabs, spans), out_shape=(j...]
    reshape x1 -> x0, local copies, waits for them, and re-layouts: 1.29 us -> none  [fused(): limits = truncation_limit.reshape(1, length)]
where the time goes in v1:
time: 46.7 us; the launch traced here: 46 us
  Pallas kernels  45.4 us (97%)
  between operations  0.64 us (1%)
    pallas_call x1, Pallas kernels, fused(): pl.pallas_call(functools.partial(fused_kernel, sizes), out_shape=(jax.Sha...  43.7 us
    pallas_call x1, Pallas kernels, fused(): pl.pallas_call(functools.partial(last_kernel, slabs, spans), out_shape=(j...  1.71 us

profile of v1, /device:TPU:1, one launch (start us, length us, event | category | flops | bytes accessed | tf_op | source)
XLA Modules:
  0.0 46.0 jit_solution(17435769448241120770)
XLA Ops:
  0.6 43.7 %fused_step.1 = (f32[304,1216]{1,0:T(8,128)S(1)}, bf16[2,304,256]{2,1,0:T(8,128)(2,1)S(1)}, bf16[2,256,1216]{2,1,0:T(8,128)(2,1)S(1)}, f32[8,128]{1,0:T(8,128)S(1)}) custom-call(f32[304,1216]{1,0:T(8,128)} %bitcast.3, s32[1216]{0:T(1024)} %limit_hbm.1, s32[2]{0:T(128)} %order_hbm.1, f32[2]{0:T(128)} %strength_hbm.1, f32[2]{0:T(128)} %mass_hbm.1, ...), custom_call_target="tpu_custom_call" | custom-call | tf_op jit(solution)/shard_map/fused_step/pallas_call | solution.py:673
  44.3 1.7 %last_product.1 = (f32[304,1216]{1,0:T(8,128)}, f32[2]{0:T(128)}, f32[1]{0:T(128)}) custom-call(f32[304,1216]{1,0:T(8,128)S(1)} %get-tuple-element.10.sum_ref, bf16[2,304,256]{2,1,0:T(8,128)(2,1)S(1)} %get-tuple-element.11.tail_ref, bf16[2,256,1216]{2,1,0:T(8,128)(2,1)S(1)} %get-tuple-element.12.tail_table, f32[8,128]{1,0:T(8,128)S(1)} %get-tuple-element.13.energy_ref), custom_call_target="tpu_custom_call" | custom-call | tf_op jit(solution)/shard_map/last_product/pallas_call | solution.py:724

commit v2 on v1

--- a/solution.py
+++ b/solution.py
@@ -174,14 +174,13 @@
 
 def fused_kernel(
     sizes,
-    grid_hbm, limit_hbm, order_hbm, strength_hbm, mass_hbm, coarse_hbm, fine_hbm,
-    back_coarse_hbm, back_fine_hbm, twiddle_hbm, base_hbm,
+    grid_hbm, limit_hbm, order_hbm, strength_hbm, mass_hbm, seeds_hbm, back_seeds_hbm, twiddle_hbm, base_hbm,
     sum_ref, tail_ref, tail_table, energy_ref,
-    grid, limit_ref, order_ref, strength_ref, mass_ref, coarse_ref, fine_ref,
-    back_coarse, back_fine, twiddle, base, grid_parts, table, back_table,
+    grid, limit_ref, order_ref, strength_ref, mass_ref, seeds, back_seeds, twiddle, base,
+    grid_parts, table, back_table,
     sent_a, sent_b, sent_c, got_a, got_b, got_c, back_a, back_b, back_c, home_a, home_b, home_c,
-    rest, work, damp, energy_sums, energy_mine, energy_wav, energy_lev,
-    load_sems, send_sems, recv_sems, local_sems, wav_send, wav_recv, lev_send, lev_recv, ready,
+    rest, work, damp, energy_sums, energy_wav, energy_lev,
+    load_sems, send_sems, recv_sems, energy_sems, ready,
 ):
     slabs, rows, length, wav, lev, quarters, columns, padded, tail, groups, group_rows, fine_rows = sizes
     half = length // 2
@@ -202,56 +201,60 @@
         def _():
             pl.semaphore_signal(barrier, inc=1, device_id=(other, me), device_id_type=MESH)
 
-    loads = [
-        pltpu.make_async_copy(src, dst, load_sems.at[n])
-        for n, (src, dst) in enumerate(
-            (
-                (coarse_hbm, coarse_ref), (fine_hbm, fine_ref), (grid_hbm, grid),
-                (limit_hbm, limit_ref), (order_hbm, order_ref), (strength_hbm, strength_ref),
-                (mass_hbm, mass_ref), (twiddle_hbm, twiddle), (base_hbm, base),
-                (back_coarse_hbm, back_coarse), (back_fine_hbm, back_fine),
-            )
-        )
-    ]
-    for load in loads:
-        load.start()
-
     def quarter_of(step):
         down, across = 1 - step % 2, 1 - step // 2
         y, x = my_quarter // 2, my_quarter % 2
         return (y + down - 2 * y * down) * 2 + (x + across - 2 * x * across)
 
-    def push(source, target, phase, w):
+    spans = [slice(at, min(at + 4 * LANES, length)) for at in range(0, length, 4 * LANES)]
+    ahead = quarter_of(0)
+    def load(source, target, sem):
+        copy = pltpu.make_async_copy(source, target, load_sems.at[sem])
+        copy.start()
+        return copy
+
+    first_load = load(seeds_hbm.at[:, ahead], seeds.at[:, quarters + 1], 0)
+    grid_loads = [load(grid_hbm.at[:, span], grid.at[:, span], 1 + n) for n, span in enumerate(spans)]
+    seeds_load = load(seeds_hbm, seeds.at[:, : quarters + 1], 1 + len(spans))
+
+    def push(source, target, phase, recv, w):
         @pl.when(w != me)
         def _():
             pltpu.make_async_remote_copy(
                 src_ref=source.at[w], dst_ref=target.at[me],
-                send_sem=send_sems.at[phase, w], recv_sem=recv_sems.at[phase, me],
+                send_sem=send_sems.at[phase], recv_sem=recv_sems.at[recv],
                 device_id=(level, w), device_id_type=MESH,
             ).start()
 
         @pl.when(w == me)
         def _():
-            pltpu.make_async_copy(source.at[w], target.at[w], local_sems.at[phase]).start()
-
-    def push_all(source, target, phase):
-        @pl.loop(0, quarters)
+            target[w] = source[w]
+
+    def push_steps(source, target, phase, recv, steps, by_step=0):
+        @pl.loop(*steps)
         def _(step):
             for slab in range(slabs):
-                push(source, target, phase, quarter_of(step) * slabs + slab)
-
-    def arrive(source, target, phase, w):
-        @pl.when(w != me)
-        def _():
-            pltpu.make_async_remote_copy(
-                src_ref=source.at[w], dst_ref=target.at[w],
-                send_sem=send_sems.at[phase, w], recv_sem=recv_sems.at[phase, w],
-                device_id=(level, w), device_id_type=MESH,
-            ).wait()
-
-        @pl.when(w == me)
-        def _():
-            pltpu.make_async_copy(source.at[w], target.at[w], local_sems.at[phase]).wait()
+                push(source, target, phase, recv + by_step * step, quarter_of(step) * slabs + slab)
+
+    def push_all(source, target, phase, recv, by_step=0):
+        push_steps(source, target, phase, recv, (0, quarters), by_step)
+
+    def batch_of(source, target, phase, recv, first, count):
+        return pltpu.make_async_remote_copy(
+            src_ref=source.at[pl.ds(first, count)], dst_ref=target.at[pl.ds(first, count)],
+            send_sem=send_sems.at[phase], recv_sem=recv_sems.at[recv],
+            device_id=(level, (me + 1) % wav), device_id_type=MESH,
+        )
+
+    def arrive_all(source, target, phase, recv):
+        batch_of(source, target, phase, recv, 0, wav - 1).wait_recv()
+
+    def arrive_step(source, target, phase, recv, step):
+        if step == quarters - 1:
+            first, count = me + 1 - 2 * my_slab, 1
+        else:
+            first, count = quarter_of(step) * slabs, slabs
+        batch_of(source, target, phase, recv + step, first, count).wait_recv()
 
     lane = lax.broadcasted_iota(jnp.int32, (1, LANES), 1)
     signs = jnp.where(lane < HALF, 1.0, -1.0)
@@ -289,48 +292,59 @@
         first = quarter % 2 * quarter_lanes
         return (first, first + part_lanes)
 
-    loads[0].wait()
-    loads[1].wait()
-
-    @pl.loop(0, quarters + 1)
-    def _(step):
-        last = step // quarters
-        piece = quarter_of(step % quarters) * (1 - last) + quarters * last
-        cos_f, sin_f = fine_ref[0, piece], fine_ref[1, piece]
+    def make_table(piece):
+        cos_f, sin_f = seeds[0, piece, :fine_rows], seeds[1, piece, :fine_rows]
 
         @pl.loop(0, length // fine_rows, unroll=2)
         def _(block):
-            cos_c, sin_c = coarse_ref[0, piece, pl.ds(block, 1)], coarse_ref[1, piece, pl.ds(block, 1)]
+            at = pl.ds(fine_rows + block, 1)
+            cos_c, sin_c = seeds[0, piece, at], seeds[1, piece, at]
             span = pl.ds(pl.multiple_of(block * fine_rows, fine_rows), fine_rows)
             value_high, value_low = halves(cos_c * cos_f - sin_c * sin_f)
             table[0, span] = value_high
             table[1, span] = value_low
 
-        @pl.when(step == 0)
-        def _():
-            loads[2].wait()
-            high, low = halves(grid[...])
-            grid_parts[0] = high
-            grid_parts[1] = low
-
-        result = product((grid_parts[0], grid_parts[1]), (table[0], table[1]))
+    def keep(result, piece):
         for slab in range(slabs):
             w = piece * slabs + slab
             sent_a[w] = result[slab * rows : (slab + 1) * rows, :LANES]
             sent_b[w] = result[slab * rows : (slab + 1) * rows, LANES:]
 
-        @pl.when(step == 0)
-        def _():
-            pl.semaphore_wait(barrier, wav - 1 + level)
+    first_load.wait()
+    make_table(quarters + 1)
+    for grid_load, span in zip(grid_loads, spans):
+        grid_load.wait()
+        high, low = halves(grid[:, span])
+        grid_parts[0, :, span] = high
+        grid_parts[1, :, span] = low
+    keep(product((grid_parts[0], grid_parts[1]), (table[0], table[1])), ahead)
+    pl.semaphore_wait(barrier, wav - 1 + level)
+    for slab in range(slabs):
+        push(sent_a, got_a, 0, 0, ahead * slabs + slab)
+
+    later = (
+        (limit_hbm, limit_ref), (order_hbm, order_ref), (strength_hbm, strength_ref), (mass_hbm, mass_ref),
+        (twiddle_hbm, twiddle), (base_hbm, base), (back_seeds_hbm, back_seeds),
+    )
+    free_sems = [n for n in range(len(later) + 1) if n != 1 + len(spans)]
+    other_loads = [load(source, target, sem) for (source, target), sem in zip(later, free_sems)]
+    seeds_load.wait()
+
+    @pl.loop(1, quarters + 1)
+    def _(step):
+        last = step // quarters
+        piece = quarter_of(step % quarters) * (1 - last) + quarters * last
+        make_table(piece)
+        keep(product((grid_parts[0], grid_parts[1]), (table[0], table[1])), piece)
 
         @pl.when(step < quarters)
         def _():
             for slab in range(slabs):
-                push(sent_a, got_a, 0, piece * slabs + slab)
+                push(sent_a, got_a, 0, 0, piece * slabs + slab)
 
         @pl.when(step == quarters - 1)
         def _():
-            push_all(sent_b, got_b, 1)
+            push_all(sent_b, got_b, 1, 1)
 
     for quarter in range(quarters):
         from_ref = sent_b if quarter // 2 else sent_a
@@ -338,15 +352,15 @@
             sent_c[quarter * slabs + slab] = pack(
                 lambda start, many: from_ref[wav + slab, start : start + many], quarter_starts(quarter)
             )
-    push_all(sent_c, got_c, 2)
+    push_all(sent_c, got_c, 2, 2)
 
     for other in range(lev - 1):
         @pl.when(other < level)
         def _():
-            pl.semaphore_signal(ready.at[level], inc=1, device_id=(other, me), device_id_type=MESH)
-
-    for load in loads[3:]:
-        load.wait()
+            pl.semaphore_signal(ready, inc=1, device_id=(other, me), device_id_type=MESH)
+
+    for other_load in other_loads:
+        other_load.wait()
     place = lax.broadcasted_iota(jnp.int32, (1, 3 * LANES), 1)
     column = place // LANES * HALF + place % HALF
     wave = my_quarter * columns + column
@@ -382,9 +396,12 @@
     blocks = LANES // fine_rows
     plain = 2 * quarters * blocks
 
+    arrivals = [quarters - 1] + list(range(quarters - 1))
+
     def back_piece(at, target, span):
-        cos_c, sin_c = back_coarse[0, pl.ds(at, 1)], back_coarse[1, pl.ds(at, 1)]
-        value_high, value_low = halves(cos_c * back_fine[0] - sin_c * back_fine[1])
+        row = pl.ds(fine_rows + at, 1)
+        cos_c, sin_c = back_seeds[0, row], back_seeds[1, row]
+        value_high, value_low = halves(cos_c * back_seeds[0, :fine_rows] - sin_c * back_seeds[1, :fine_rows])
         target[0, span] = value_high
         target[1, span] = value_low
 
@@ -395,9 +412,12 @@
             span = pl.ds(pl.multiple_of(block * fine_rows, fine_rows), fine_rows)
             back_piece(n * blocks + block, back_table.at[n], span)
 
-    @pl.loop(0, 2 * blocks)
-    def _(block):
-        back_piece(plain + block, tail_table, pl.ds(pl.multiple_of(block * fine_rows, fine_rows), fine_rows))
+    for place_of, step in enumerate(arrivals):
+        for part in range(2):
+            block = 2 * place_of + part
+            back_piece(
+                plain + 2 * quarter_of(step) + part, tail_table, slice(block * fine_rows, (block + 1) * fine_rows)
+            )
 
     sum_ref[...] = jnp.zeros_like(sum_ref)
     energy_sums[...] = jnp.zeros_like(energy_sums)
@@ -411,12 +431,8 @@
     batch = 2
 
     def in_blocks(body):
-        @pl.loop(0, rows // block_rows)
-        def _(block):
-            body(pl.multiple_of(block * block_rows, 8), block_rows)
-
-        if rows % block_rows:
-            body(rows - rows % block_rows, rows % block_rows)
+        for start in range(0, rows, block_rows):
+            body(start, min(block_rows, rows - start))
 
     def middle(tile, source, target):
         span_of = slice(tile * LANES, (tile + 1) * LANES)
@@ -465,46 +481,40 @@
 
         in_blocks(join)
 
-    def wav_copy(target, slot):
+    def wav_copy(target, slot, count=1):
         return pltpu.make_async_remote_copy(
-            src_ref=energy_mine, dst_ref=energy_wav.at[slot],
-            send_sem=wav_send.at[target], recv_sem=wav_recv.at[slot],
+            src_ref=energy_wav.at[pl.ds(slot, count)], dst_ref=energy_wav.at[pl.ds(slot, count)],
+            send_sem=energy_sems.at[0], recv_sem=energy_sems.at[1],
             device_id=(level, target), device_id_type=MESH,
         )
 
-    def lev_copy(target, slot):
+    def lev_copy(target, slot, count=1):
         return pltpu.make_async_remote_copy(
-            src_ref=energy_lev.at[level], dst_ref=energy_lev.at[slot],
-            send_sem=lev_send.at[target], recv_sem=lev_recv.at[slot],
+            src_ref=energy_lev.at[pl.ds(slot, count)], dst_ref=energy_lev.at[pl.ds(slot, count)],
+            send_sem=energy_sems.at[2], recv_sem=energy_sems.at[3],
             device_id=(target, me), device_id_type=MESH,
         )
 
     def announce():
-        mine = jnp.sum(energy_sums[...], axis=0, keepdims=True)
-        energy_mine[...] = mine
-        energy_wav[me] = mine
+        energy_wav[me] = jnp.sum(energy_sums[...], axis=0, keepdims=True)
 
         @pl.loop(1, wav)
         def _(step):
             wav_copy((me + step) % wav, me).start()
 
+        push_steps(back_b, home_b, 4, 4, (1, quarters - 1), 1)
+
+    arrive_all(sent_a, got_a, 0, 0)
+    middle(0, got_a, back_a)
+    push_all(back_a, home_a, 3, 3)
+    arrive_all(sent_b, got_b, 1, 1)
+    middle(1, got_b, back_b)
+    push_steps(back_b, home_b, 4, 4, (0, 1), 1)
+    push_steps(back_b, home_b, 4, 4, (quarters - 1, quarters), 1)
+    arrive_all(sent_c, got_c, 2, 2)
+
     @pl.loop(0, wav)
     def _(w):
-        arrive(sent_a, got_a, 0, w)
-
-    middle(0, got_a, back_a)
-    push_all(back_a, home_a, 3)
-
-    @pl.loop(0, wav)
-    def _(w):
-        arrive(sent_b, got_b, 1, w)
-
-    middle(1, got_b, back_b)
-    push_all(back_b, home_b, 4)
-
-    @pl.loop(0, wav)
-    def _(w):
-        arrive(sent_c, got_c, 2, w)
         rest[w] = unpack(got_c[w], wide)
 
     middle(2, rest, rest)
@@ -514,32 +524,25 @@
         for slab in range(slabs):
             w = quarter_of(step) * slabs + slab
             back_c[w] = pack(lambda start, many: rest[w, start : start + many], wide)
-            push(back_c, home_c, 5, w)
-
-    def finish(tile, phase, back, home):
-        @pl.loop(0, quarters // 2)
-        def _(pair):
-            found, right = [], ([], [])
-            for n in range(2):
-                quarter = quarter_of((2 * pair + n + quarters - 1) % quarters)
-                stacked = []
-                for slab in range(slabs):
-                    w = quarter * slabs + slab
-                    arrive(back, home, phase, w)
-                    stacked.append(home[w])
-                found.append(jnp.concatenate(stacked, 0))
-                for part in range(2):
-                    right[part].append(back_table[tile * quarters + quarter, part])
-            left = halves(jnp.concatenate(found, 1))
-            sum_ref[...] += product(left, [jnp.concatenate(part, 0) for part in right])
-
-    finish(0, 3, back_a, home_a)
-    finish(1, 4, back_b, home_b)
-
-    @pl.loop(1, wav)
+            push(back_c, home_c, 5, 4 + quarters + step, w)
+
+    def add_pair(tile, home, steps):
+        found, right = [], ([], [])
+        for step in steps:
+            quarter = quarter_of(step)
+            found.append(jnp.concatenate([home[quarter * slabs + slab] for slab in range(slabs)], 0))
+            for part in range(2):
+                right[part].append(back_table[tile * quarters + quarter, part])
+        left = halves(jnp.concatenate(found, 1))
+        sum_ref[...] += product(left, [jnp.concatenate(part, 0) for part in right])
+
+    arrive_all(back_a, home_a, 3, 3)
+
+    @pl.loop(0, quarters, step=2)
     def _(step):
-        source = (me + step) % wav
-        wav_copy(source, source).wait()
+        add_pair(0, home_a, (step, step + 1))
+
+    wav_copy((me + 1) % wav, 0, wav - 1).wait()
 
     slab_sums = []
     for slab in range(slabs):
@@ -552,35 +555,38 @@
         weighted = weighted + slab_sums[slab] * mass_ref[slab]
     energy_lev[level] = weighted
 
-    for other in range(1, lev):
-        @pl.when(level < other)
-        def _():
-            pl.semaphore_wait(ready.at[other], 1)
+    @pl.when(level < lev - 1)
+    def _():
+        pl.semaphore_wait(ready, lev - 1 - level)
 
     for other in range(lev):
         @pl.when(level != other)
         def _():
             lev_copy(other, level).start()
 
-    @pl.loop(0, wav)
-    def _(w):
-        arrive(back_c, home_c, 5, w)
+    for pair in range(0, quarters, 2):
+        for step in arrivals[pair : pair + 2]:
+            arrive_step(back_b, home_b, 4, 4, step)
+        add_pair(1, home_b, arrivals[pair : pair + 2])
 
     for side in range(2):
+        values = [jnp.zeros((rows, LANES), jnp.float32)] * slabs
+        for place_of in range(2 * side, 2 * side + 2):
+            arrive_step(back_c, home_c, 5, 4 + quarters, arrivals[place_of])
+            for slab in range(slabs):
+                w = quarter_of(arrivals[place_of]) * slabs + slab
+                values[slab] = values[slab] + unpack(home_c[w], quarter_starts(place_of))
         for slab in range(slabs):
-            value = sum(
-                unpack(home_c[quarter * slabs + slab], quarter_starts(quarter))
-                for quarter in range(2 * side, 2 * side + 2)
-            )
-            value_high, value_low = halves(value)
+            value_high, value_low = halves(values[slab])
             at = (slice(slab * rows, (slab + 1) * rows), slice(side * LANES, (side + 1) * LANES))
             tail_ref[(0,) + at] = value_high
             tail_ref[(1,) + at] = value_low
 
-    for other in range(lev):
-        @pl.when(level != other)
-        def _():
-            lev_copy(other, other).wait()
+    for phase, (source, target) in enumerate(
+        ((sent_a, got_a), (sent_b, got_b), (sent_c, got_c), (back_a, home_a), (back_b, home_b), (back_c, home_c))
+    ):
+        batch_of(source, target, phase, 0, 0, wav - 1).wait_send()
+    lev_copy((level + 1) % lev, 0, lev - 1).wait()
 
     total = energy_lev[0]
     for other in range(1, lev):
@@ -646,15 +652,27 @@
     near = np.arange(fine_rows)
     positions = np.arange(length)
     single = lambda array: jnp.asarray(array, jnp.float32)
-    coarse = single(cos_sin(steps[None, :, None] * waves[:, None, :], length))
-    fine = single(cos_sin(near[None, :, None] * waves[:, None, :] + phase[:, None, :], length))
+    seeds = single(
+        np.concatenate(
+            [
+                cos_sin(near[None, :, None] * waves[:, None, :] + phase[:, None, :], length),
+                cos_sin(steps[None, :, None] * waves[:, None, :], length),
+            ],
+            2,
+        )
+    )
     by_tile = lambda array: np.concatenate(
         [array[:quarters, :LANES].ravel(), array[:quarters, LANES:].ravel(), array[quarters]]
     )[::fine_rows]
-    back_coarse = single(
-        cos_sin(by_tile(waves)[:, None] * positions[None] + by_tile(phase)[:, None], length)
-    )
-    back_fine = single(cos_sin(near[:, None] * positions[None], length))
+    back_seeds = single(
+        np.concatenate(
+            [
+                cos_sin(near[:, None] * positions[None], length),
+                cos_sin(by_tile(waves)[:, None] * positions[None] + by_tile(phase)[:, None], length),
+            ],
+            1,
+        )
+    )
     inner = np.arange(padded)
     turns = cos_sin(np.arange(wav)[:, None, None] * inner[None, :, None], length)
     twiddle = single(np.repeat(turns, HALF, 3).transpose(1, 2, 0, 3).reshape(wav, padded, LANES))
@@ -678,7 +696,7 @@
             jax.ShapeDtypeStruct((2, 2 * LANES, length), bf16),
             jax.ShapeDtypeStruct((8, LANES), f32),
         ),
-        in_specs=[hbm] * 11,
+        in_specs=[hbm] * 9,
         out_specs=(vmem,) * 4,
         scratch_shapes=[
             pltpu.VMEM((slabs * rows, length), f32),
@@ -686,10 +704,8 @@
             pltpu.SMEM((slabs,), i32),
             pltpu.SMEM((slabs,), f32),
             pltpu.SMEM((slabs,), f32),
-            pltpu.VMEM(coarse.shape, f32),
-            pltpu.VMEM(fine.shape, f32),
-            pltpu.VMEM(back_coarse.shape, f32),
-            pltpu.VMEM(back_fine.shape, f32),
+            pltpu.VMEM((2, quarters + 2) + seeds.shape[2:], f32),
+            pltpu.VMEM(back_seeds.shape, f32),
             pltpu.VMEM(twiddle.shape, f32),
             pltpu.VMEM(base.shape, bf16),
             pltpu.VMEM((2, slabs * rows, length), bf16),
@@ -700,12 +716,10 @@
             pltpu.VMEM((wav, padded, LANES), f32),
             pltpu.VMEM((wav, padded, 3 * LANES), f32),
             pltpu.VMEM((8, LANES), f32),
-            pltpu.VMEM((1, LANES), f32),
             pltpu.VMEM((wav, 1, LANES), f32),
             pltpu.VMEM((lev, 1, LANES), f32),
-            dma((11,)), dma((6, wav)), dma((6, wav)), dma((6,)),
-            dma((wav,)), dma((wav,)), dma((lev,)), dma((lev,)),
-            pltpu.SemaphoreType.REGULAR((lev,)),
+            dma((8,)), dma((6,)), dma((4 + 2 * quarters,)), dma((4,)),
+            pltpu.SemaphoreType.REGULAR,
         ],
         compiler_params=pltpu.CompilerParams(
             collective_id=0, has_side_effects=True, vmem_limit_bytes=40 * 1024 * 1024
@@ -716,7 +730,7 @@
             pltpu.with_memory_space_constraint(array, pltpu.HBM)
             for array in (
                 grid_field.reshape(slabs * rows, length), truncation_limit, diffusion_order,
-                diffusion_strength, mass_weight, coarse, fine, back_coarse, back_fine, twiddle, base,
+                diffusion_strength, mass_weight, seeds, back_seeds, twiddle, base,
             )
         )
     )

time: 46.7 us -> 42 us (0.90)
  Pallas kernels: 45.4 us -> 41 us
    pallas_call x1, Pallas kernels: 43.7 us -> 39.3 us  [fused(): pl.pallas_call(functools.partial(fused_kernel, sizes), out_shape=(jax.Sha...]
where the time goes in v2:
time: 42 us; the launch traced here: 41.7 us
  Pallas kernels  41 us (98%)
  between operations  0.64 us (2%)
    pallas_call x1, Pallas kernels, fused(): pl.pallas_call(functools.partial(fused_kernel, sizes), out_shape=(jax.Sha...  39.3 us
    pallas_call x1, Pallas kernels, fused(): pl.pallas_call(functools.partial(last_kernel, slabs, spans), out_shape=(j...  1.71 us

profile of v2, /device:TPU:1, one launch (start us, length us, event | category | flops | bytes accessed | tf_op | source)
XLA Modules:
  0.0 41.7 jit_solution(9759854885320778413)
XLA Ops:
  0.6 39.3 %fused_step.1 = (f32[304,1216]{1,0:T(8,128)S(1)}, bf16[2,304,256]{2,1,0:T(8,128)(2,1)S(1)}, bf16[2,256,1216]{2,1,0:T(8,128)(2,1)S(1)}, f32[8,128]{1,0:T(8,128)S(1)}) custom-call(f32[304,1216]{1,0:T(8,128)} %bitcast.3, s32[1216]{0:T(1024)} %limit_hbm.1, s32[2]{0:T(128)} %order_hbm.1, f32[2]{0:T(128)} %strength_hbm.1, f32[2]{0:T(128)} %mass_hbm.1, ...), custom_call_target="tpu_custom_call" | custom-call | tf_op jit(solution)/shard_map/fused_step/pallas_call | solution.py:691
  40.0 1.7 %last_product.1 = (f32[304,1216]{1,0:T(8,128)}, f32[2]{0:T(128)}, f32[1]{0:T(128)}) custom-call(f32[304,1216]{1,0:T(8,128)S(1)} %get-tuple-element.10.sum_ref, bf16[2,304,256]{2,1,0:T(8,128)(2,1)S(1)} %get-tuple-element.11.tail_ref, bf16[2,256,1216]{2,1,0:T(8,128)(2,1)S(1)} %get-tuple-element.12.tail_table, f32[8,128]{1,0:T(8,128)S(1)} %get-tuple-element.13.energy_ref), custom_call_target="tpu_custom_call" | custom-call | tf_op jit(solution)/shard_map/last_product/pallas_call | solution.py:738

commit v3 on v2

--- a/solution.py
+++ b/solution.py
@@ -192,21 +192,13 @@
 
     barrier = pltpu.get_barrier_semaphore()
 
-    @pl.loop(1, wav)
-    def _(step):
-        pl.semaphore_signal(barrier, inc=1, device_id=(level, (me + step) % wav), device_id_type=MESH)
-
-    for other in range(1, lev):
-        @pl.when(level < other)
-        def _():
-            pl.semaphore_signal(barrier, inc=1, device_id=(other, me), device_id_type=MESH)
-
     def quarter_of(step):
         down, across = 1 - step % 2, 1 - step // 2
         y, x = my_quarter // 2, my_quarter % 2
         return (y + down - 2 * y * down) * 2 + (x + across - 2 * x * across)
 
-    spans = [slice(at, min(at + 4 * LANES, length)) for at in range(0, length, 4 * LANES)]
+    early = -(-rows // 16) * 16
+    spans = [slice(0, early), slice(early, slabs * rows)]
     ahead = quarter_of(0)
     def load(source, target, sem):
         copy = pltpu.make_async_copy(source, target, load_sems.at[sem])
@@ -214,8 +206,17 @@
         return copy
 
     first_load = load(seeds_hbm.at[:, ahead], seeds.at[:, quarters + 1], 0)
-    grid_loads = [load(grid_hbm.at[:, span], grid.at[:, span], 1 + n) for n, span in enumerate(spans)]
+    grid_loads = [load(grid_hbm.at[span], grid.at[span], 1 + n) for n, span in enumerate(spans)]
     seeds_load = load(seeds_hbm, seeds.at[:, : quarters + 1], 1 + len(spans))
+
+    @pl.loop(1, wav)
+    def _(step):
+        pl.semaphore_signal(barrier, inc=1, device_id=(level, (me + step) % wav), device_id_type=MESH)
+
+    for other in range(1, lev):
+        @pl.when(level < other)
+        def _():
+            pl.semaphore_signal(barrier, inc=1, device_id=(other, me), device_id_type=MESH)
 
     def push(source, target, phase, recv, w):
         @pl.when(w != me)
@@ -230,14 +231,14 @@
         def _():
             target[w] = source[w]
 
-    def push_steps(source, target, phase, recv, steps, by_step=0):
-        @pl.loop(*steps)
+    def push_quarter(source, target, phase, recv, quarter):
+        for n in range(slabs):
+            push(source, target, phase, recv, quarter * slabs + n)
+
+    def push_all(source, target, phase, recv, by_step=0):
+        @pl.loop(0, quarters)
         def _(step):
-            for slab in range(slabs):
-                push(source, target, phase, recv + by_step * step, quarter_of(step) * slabs + slab)
-
-    def push_all(source, target, phase, recv, by_step=0):
-        push_steps(source, target, phase, recv, (0, quarters), by_step)
+            push_quarter(source, target, phase, recv + by_step * step, quarter_of(step))
 
     def batch_of(source, target, phase, recv, first, count):
         return pltpu.make_async_remote_copy(
@@ -292,17 +293,17 @@
         first = quarter % 2 * quarter_lanes
         return (first, first + part_lanes)
 
-    def make_table(piece):
-        cos_f, sin_f = seeds[0, piece, :fine_rows], seeds[1, piece, :fine_rows]
+    def make_table(piece, lanes):
+        cos_f, sin_f = seeds[0, piece, :fine_rows, lanes], seeds[1, piece, :fine_rows, lanes]
 
         @pl.loop(0, length // fine_rows, unroll=2)
         def _(block):
             at = pl.ds(fine_rows + block, 1)
-            cos_c, sin_c = seeds[0, piece, at], seeds[1, piece, at]
+            cos_c, sin_c = seeds[0, piece, at][:, lanes], seeds[1, piece, at][:, lanes]
             span = pl.ds(pl.multiple_of(block * fine_rows, fine_rows), fine_rows)
             value_high, value_low = halves(cos_c * cos_f - sin_c * sin_f)
-            table[0, span] = value_high
-            table[1, span] = value_low
+            table[0, span, lanes] = value_high
+            table[1, span, lanes] = value_low
 
     def keep(result, piece):
         for slab in range(slabs):
@@ -310,17 +311,30 @@
             sent_a[w] = result[slab * rows : (slab + 1) * rows, :LANES]
             sent_b[w] = result[slab * rows : (slab + 1) * rows, LANES:]
 
+    front, behind = slice(0, LANES), slice(LANES, 2 * LANES)
     first_load.wait()
-    make_table(quarters + 1)
-    for grid_load, span in zip(grid_loads, spans):
-        grid_load.wait()
-        high, low = halves(grid[:, span])
-        grid_parts[0, :, span] = high
-        grid_parts[1, :, span] = low
-    keep(product((grid_parts[0], grid_parts[1]), (table[0], table[1])), ahead)
+    make_table(quarters + 1, front)
+
+    def first_rows(span):
+        high, low = halves(grid[span])
+        grid_parts[0, span] = high
+        grid_parts[1, span] = low
+        return product((grid_parts[0, span], grid_parts[1, span]), (table[0, :, front], table[1, :, front]))
+
+    grid_loads[0].wait()
+    result = first_rows(spans[0])
+    sent_a[ahead * slabs] = result[:rows]
+    if early > rows:
+        sent_a[ahead * slabs + 1, : early - rows] = result[rows:]
     pl.semaphore_wait(barrier, wav - 1 + level)
+    push(sent_a, got_a, 0, 0, ahead * slabs)
+    grid_loads[1].wait()
+    sent_a[ahead * slabs + 1, early - rows :] = first_rows(spans[1])
+    push(sent_a, got_a, 0, 0, ahead * slabs + 1)
+    make_table(quarters + 1, behind)
+    result = product((grid_parts[0], grid_parts[1]), (table[0, :, behind], table[1, :, behind]))
     for slab in range(slabs):
-        push(sent_a, got_a, 0, 0, ahead * slabs + slab)
+        sent_b[ahead * slabs + slab] = result[slab * rows : (slab + 1) * rows]
 
     later = (
         (limit_hbm, limit_ref), (order_hbm, order_ref), (strength_hbm, strength_ref), (mass_hbm, mass_ref),
@@ -330,29 +344,30 @@
     other_loads = [load(source, target, sem) for (source, target), sem in zip(later, free_sems)]
     seeds_load.wait()
 
-    @pl.loop(1, quarters + 1)
+    @pl.loop(0, quarters)
     def _(step):
-        last = step // quarters
-        piece = quarter_of(step % quarters) * (1 - last) + quarters * last
-        make_table(piece)
+        plain_step = (step + quarters - 1) // quarters
+        piece = quarter_of(step) * plain_step + quarters * (1 - plain_step)
+        make_table(piece, slice(0, 2 * LANES))
         keep(product((grid_parts[0], grid_parts[1]), (table[0], table[1])), piece)
 
-        @pl.when(step < quarters)
+        @pl.when(step == 0)
         def _():
-            for slab in range(slabs):
-                push(sent_a, got_a, 0, 0, piece * slabs + slab)
+            for quarter in range(quarters):
+                from_ref = sent_b if quarter // 2 else sent_a
+                for slab in range(slabs):
+                    sent_c[quarter * slabs + slab] = pack(
+                        lambda start, many: from_ref[wav + slab, start : start + many], quarter_starts(quarter)
+                    )
+            push_all(sent_c, got_c, 2, 2)
+
+        @pl.when(step > 0)
+        def _():
+            push_quarter(sent_a, got_a, 0, 0, piece)
 
         @pl.when(step == quarters - 1)
         def _():
             push_all(sent_b, got_b, 1, 1)
-
-    for quarter in range(quarters):
-        from_ref = sent_b if quarter // 2 else sent_a
-        for slab in range(slabs):
-            sent_c[quarter * slabs + slab] = pack(
-                lambda start, many: from_ref[wav + slab, start : start + many], quarter_starts(quarter)
-            )
-    push_all(sent_c, got_c, 2, 2)
 
     for other in range(lev - 1):
         @pl.when(other < level)
@@ -471,7 +486,7 @@
         sums = sum(sums[:, n * LANES : (n + 1) * LANES] for n in range(batch))
         energy_sums[...] += sums * energy_weight[:, span_of]
 
-        if tile == 2:
+        if tile == 1:
             announce()
 
         def join(start, many):
@@ -502,29 +517,25 @@
         def _(step):
             wav_copy((me + step) % wav, me).start()
 
-        push_steps(back_b, home_b, 4, 4, (1, quarters - 1), 1)
+    arrive_all(sent_c, got_c, 2, 2)
+
+    @pl.loop(0, wav)
+    def _(w):
+        rest[w] = unpack(got_c[w], wide)
+
+    middle(2, rest, rest)
+
+    @pl.loop(0, wav)
+    def _(w):
+        back_c[w] = pack(lambda start, many: rest[w, start : start + many], wide)
 
     arrive_all(sent_a, got_a, 0, 0)
     middle(0, got_a, back_a)
     push_all(back_a, home_a, 3, 3)
     arrive_all(sent_b, got_b, 1, 1)
     middle(1, got_b, back_b)
-    push_steps(back_b, home_b, 4, 4, (0, 1), 1)
-    push_steps(back_b, home_b, 4, 4, (quarters - 1, quarters), 1)
-    arrive_all(sent_c, got_c, 2, 2)
-
-    @pl.loop(0, wav)
-    def _(w):
-        rest[w] = unpack(got_c[w], wide)
-
-    middle(2, rest, rest)
-
-    @pl.loop(0, quarters)
-    def _(step):
-        for slab in range(slabs):
-            w = quarter_of(step) * slabs + slab
-            back_c[w] = pack(lambda start, many: rest[w, start : start + many], wide)
-            push(back_c, home_c, 5, 4 + quarters + step, w)
+    push_all(back_b, home_b, 4, 4, 1)
+    push_all(back_c, home_c, 5, 4 + quarters, 1)
 
     def add_pair(tile, home, steps):
         found, right = [], ([], [])
@@ -569,9 +580,20 @@
             arrive_step(back_b, home_b, 4, 4, step)
         add_pair(1, home_b, arrivals[pair : pair + 2])
 
+    def collect_energies():
+        lev_copy((level + 1) % lev, 0, lev - 1).wait()
+
+        total = energy_lev[0]
+        for other in range(1, lev):
+            total = total + energy_lev[other]
+        fill = jnp.zeros((8 - slabs - 1, LANES), jnp.float32)
+        energy_ref[...] = jnp.concatenate(slab_sums + [total / (lev * slabs), fill], 0)
+
     for side in range(2):
         values = [jnp.zeros((rows, LANES), jnp.float32)] * slabs
         for place_of in range(2 * side, 2 * side + 2):
+            if place_of == quarters - 1:
+                collect_energies()
             arrive_step(back_c, home_c, 5, 4 + quarters, arrivals[place_of])
             for slab in range(slabs):
                 w = quarter_of(arrivals[place_of]) * slabs + slab
@@ -586,38 +608,37 @@
         ((sent_a, got_a), (sent_b, got_b), (sent_c, got_c), (back_a, home_a), (back_b, home_b), (back_c, home_c))
     ):
         batch_of(source, target, phase, 0, 0, wav - 1).wait_send()
-    lev_copy((level + 1) % lev, 0, lev - 1).wait()
-
-    total = energy_lev[0]
-    for other in range(1, lev):
-        total = total + energy_lev[other]
-    fill = jnp.zeros((8 - slabs - 1, LANES), jnp.float32)
-    energy_ref[...] = jnp.concatenate(slab_sums + [total / (lev * slabs), fill], 0)
 
 
 def last_kernel(
     slabs, spans, sum_ref, tail_ref, tail_table, energy_ref, out_hbm, energies_hbm, total_hbm,
     out, energies, total, sems,
 ):
+    copies = []
+
+    def send(source, target):
+        copies.append(pltpu.make_async_copy(source, target, sems.at[len(copies)]))
+        copies[-1].start()
+
+    def ready(span):
+        return product((tail_ref[0], tail_ref[1]), (tail_table[0, :, span], tail_table[1, :, span]))
+
+    def write(span, value):
+        out[:, span] = sum_ref[:, span] + value
+        send(out.at[:, span], out_hbm.at[:, span])
+
+    held = ready(spans[0])
+    for n in range(1, len(spans)):
+        following = ready(spans[n])
+        write(spans[n - 1], held)
+        held = following
+    write(spans[-1], held)
     sums = jnp.sum(energy_ref[...], axis=1, keepdims=True)
     for slab in range(slabs):
         energies[slab] = sums[slab, 0]
     total[0] = sums[slabs, 0]
-    copies = [
-        pltpu.make_async_copy(energies, energies_hbm, sems.at[0]),
-        pltpu.make_async_copy(total, total_hbm, sems.at[1]),
-    ]
-    for copy in copies:
-        copy.start()
-    left = (tail_ref[0], tail_ref[1])
-    for n, (start, stop) in enumerate(spans):
-        out[:, start:stop] = sum_ref[:, start:stop] + product(
-            left, (tail_table[0, :, start:stop], tail_table[1, :, start:stop])
-        )
-        copies.append(
-            pltpu.make_async_copy(out.at[:, start:stop], out_hbm.at[:, start:stop], sems.at[2 + n])
-        )
-        copies[-1].start()
+    send(energies, energies_hbm)
+    send(total, total_hbm)
     for copy in copies:
         copy.wait()
 
@@ -734,7 +755,7 @@
             )
         )
     )
-    spans = [(at, min(at + 2 * LANES, length)) for at in range(0, length, 2 * LANES)]
+    spans = [slice(at, min(at + 2 * LANES, length)) for at in range(0, length, 2 * LANES)]
     filtered, energies, total = pl.pallas_call(
         functools.partial(last_kernel, slabs, spans),
         out_shape=(

time: 42 us -> 41.2 us (0.981)
  Pallas kernels: 41 us -> 40.2 us
    pallas_call x1, Pallas kernels: 39.3 us -> 38.5 us  [fused(): pl.pallas_call(functools.partial(fused_kernel, sizes), out_shape=(jax.Sha...]
where the time goes in v3:
time: 41.2 us; the launch traced here: 41 us
  Pallas kernels  40.2 us (98%)
  between operations  0.8 us (2%)
    pallas_call x1, Pallas kernels, fused(): pl.pallas_call(functools.partial(fused_kernel, sizes), out_shape=(jax.Sha...  38.5 us
    pallas_call x1, Pallas kernels, fused(): pl.pallas_call(functools.partial(last_kernel, slabs, spans), out_shape=(j...  1.73 us

profile of v3, /device:TPU:1, one launch (start us, length us, event | category | flops | bytes accessed | tf_op | source)
XLA Modules:
  0.0 41.0 jit_solution(11682553042112855445)
XLA Ops:
  0.6 38.5 %fused_step.1 = (f32[304,1216]{1,0:T(8,128)S(1)}, bf16[2,304,256]{2,1,0:T(8,128)(2,1)S(1)}, bf16[2,256,1216]{2,1,0:T(8,128)(2,1)S(1)}, f32[8,128]{1,0:T(8,128)S(1)}) custom-call(f32[304,1216]{1,0:T(8,128)} %bitcast.3, s32[1216]{0:T(1024)} %limit_hbm.1, s32[2]{0:T(128)} %order_hbm.1, f32[2]{0:T(128)} %strength_hbm.1, f32[2]{0:T(128)} %mass_hbm.1, ...), custom_call_target="tpu_custom_call" | custom-call | tf_op jit(solution)/shard_map/fused_step/pallas_call | solution.py:712
  39.1 1.7 %last_product.1 = (f32[304,1216]{1,0:T(8,128)}, f32[2]{0:T(128)}, f32[1]{0:T(128)}) custom-call(f32[304,1216]{1,0:T(8,128)S(1)} %get-tuple-element.10.sum_ref, bf16[2,304,256]{2,1,0:T(8,128)(2,1)S(1)} %get-tuple-element.11.tail_ref, bf16[2,256,1216]{2,1,0:T(8,128)(2,1)S(1)} %get-tuple-element.12.tail_table, f32[8,128]{1,0:T(8,128)S(1)} %get-tuple-element.13.energy_ref), custom_call_target="tpu_custom_call" | custom-call | tf_op jit(solution)/shard_map/last_product/pallas_call | solution.py:759

commit v4 on v3

--- a/solution.py
+++ b/solution.py
@@ -131,8 +131,9 @@
 
 
 def product(left, right):
-    dot = functools.partial(jnp.dot, preferred_element_type=jnp.float32)
-    return dot(left[0], right[0]) + dot(left[1], right[0]) + dot(left[0], right[1])
+    left = jnp.concatenate([left[0], left[1], left[0]], 1)
+    right = jnp.concatenate([right[0], right[0], right[1]], 0)
+    return jnp.dot(left, right, preferred_element_type=jnp.float32)
 
 
 def swap(value):
@@ -172,12 +173,29 @@
     return found
 
 
+def store_circle(target, span, steps, length):
+    steps = steps.astype(jnp.float32)
+    turn = jnp.floor(steps * (4.0 / length) + 0.5)
+    angle = (steps - turn * (length // 4)) * (2.0 * np.pi / length)
+    square = angle * angle
+    cosine, sine = jnp.ones_like(angle), jnp.ones_like(angle)
+    for n in range(10, 0, -2):
+        cosine = 1.0 - cosine * square * (1.0 / (n * (n - 1)))
+        sine = 1.0 - sine * square * (1.0 / (n * (n + 1)))
+    sine = sine * angle
+    quadrant = turn.astype(jnp.int32) % 4
+    odd = quadrant % 2 == 1
+    cos_part, sin_part = jnp.where(odd, sine, cosine), jnp.where(odd, cosine, sine)
+    target[0, 0, span] = jnp.where((quadrant == 1) | (quadrant == 2), -cos_part, cos_part)
+    target[1, 0, span] = jnp.where(quadrant >= 2, -sin_part, sin_part)
+
+
 def fused_kernel(
     sizes,
     grid_hbm, limit_hbm, order_hbm, strength_hbm, mass_hbm, seeds_hbm, back_seeds_hbm, twiddle_hbm, base_hbm,
     sum_ref, tail_ref, tail_table, energy_ref,
-    grid, limit_ref, order_ref, strength_ref, mass_ref, seeds, back_seeds, twiddle, base,
-    grid_parts, table, back_table,
+    grid, limit_ref, order_ref, strength_ref, mass_ref, seeds, first_seeds, back_seeds, twiddle, base,
+    grid_parts, table, back_table, near_table,
     sent_a, sent_b, sent_c, got_a, got_b, got_c, back_a, back_b, back_c, home_a, home_b, home_c,
     rest, work, damp, energy_sums, energy_wav, energy_lev,
     load_sems, send_sems, recv_sems, energy_sems, ready,
@@ -205,9 +223,8 @@
         copy.start()
         return copy
 
-    first_load = load(seeds_hbm.at[:, ahead], seeds.at[:, quarters + 1], 0)
-    grid_loads = [load(grid_hbm.at[span], grid.at[span], 1 + n) for n, span in enumerate(spans)]
-    seeds_load = load(seeds_hbm, seeds.at[:, : quarters + 1], 1 + len(spans))
+    grid_loads = [load(grid_hbm.at[span], grid.at[span], n) for n, span in enumerate(spans)]
+    seeds_load = load(seeds_hbm, seeds, len(spans))
 
     @pl.loop(1, wav)
     def _(step):
@@ -235,10 +252,14 @@
         for n in range(slabs):
             push(source, target, phase, recv, quarter * slabs + n)
 
-    def push_all(source, target, phase, recv, by_step=0):
+    def push_all(source, target, phase, recv):
         @pl.loop(0, quarters)
         def _(step):
-            push_quarter(source, target, phase, recv + by_step * step, quarter_of(step))
+            push_quarter(source, target, phase, recv, quarter_of(step))
+
+    def push_steps(source, target, phase, recv, steps):
+        for step in steps:
+            push_quarter(source, target, phase, recv, quarter_of(step))
 
     def batch_of(source, target, phase, recv, first, count):
         return pltpu.make_async_remote_copy(
@@ -247,15 +268,11 @@
             device_id=(level, (me + 1) % wav), device_id_type=MESH,
         )
 
-    def arrive_all(source, target, phase, recv):
-        batch_of(source, target, phase, recv, 0, wav - 1).wait_recv()
-
-    def arrive_step(source, target, phase, recv, step):
-        if step == quarters - 1:
-            first, count = me + 1 - 2 * my_slab, 1
-        else:
-            first, count = quarter_of(step) * slabs, slabs
-        batch_of(source, target, phase, recv + step, first, count).wait_recv()
+    def arrive(source, target, phase, recv, count):
+        batch_of(source, target, phase, recv, 0, count).wait_recv()
+
+    def sent_all(source, target, phase):
+        batch_of(source, target, phase, 0, 0, wav - 1).wait_send()
 
     lane = lax.broadcasted_iota(jnp.int32, (1, LANES), 1)
     signs = jnp.where(lane < HALF, 1.0, -1.0)
@@ -293,13 +310,13 @@
         first = quarter % 2 * quarter_lanes
         return (first, first + part_lanes)
 
-    def make_table(piece, lanes):
-        cos_f, sin_f = seeds[0, piece, :fine_rows, lanes], seeds[1, piece, :fine_rows, lanes]
+    def make_table(start, piece, lanes):
+        cos_f, sin_f = start[0, piece, :fine_rows, lanes], start[1, piece, :fine_rows, lanes]
 
         @pl.loop(0, length // fine_rows, unroll=2)
         def _(block):
             at = pl.ds(fine_rows + block, 1)
-            cos_c, sin_c = seeds[0, piece, at][:, lanes], seeds[1, piece, at][:, lanes]
+            cos_c, sin_c = start[0, piece, at][:, lanes], start[1, piece, at][:, lanes]
             span = pl.ds(pl.multiple_of(block * fine_rows, fine_rows), fine_rows)
             value_high, value_low = halves(cos_c * cos_f - sin_c * sin_f)
             table[0, span, lanes] = value_high
@@ -312,8 +329,12 @@
             sent_b[w] = result[slab * rows : (slab + 1) * rows, LANES:]
 
     front, behind = slice(0, LANES), slice(LANES, 2 * LANES)
-    first_load.wait()
-    make_table(quarters + 1, front)
+    ahead_wave = ahead * columns + lane % HALF
+    nearby = lax.broadcasted_iota(jnp.int32, (fine_rows, 1), 0)
+    afar = lax.broadcasted_iota(jnp.int32, (length // fine_rows, 1), 0) * fine_rows
+    store_circle(first_seeds, slice(0, fine_rows), nearby * ahead_wave + lane // HALF * (length // 4), length)
+    store_circle(first_seeds, slice(fine_rows, fine_rows + length // fine_rows), afar * ahead_wave, length)
+    make_table(first_seeds, 0, front)
 
     def first_rows(span):
         high, low = halves(grid[span])
@@ -331,7 +352,8 @@
     grid_loads[1].wait()
     sent_a[ahead * slabs + 1, early - rows :] = first_rows(spans[1])
     push(sent_a, got_a, 0, 0, ahead * slabs + 1)
-    make_table(quarters + 1, behind)
+    seeds_load.wait()
+    make_table(seeds, ahead, behind)
     result = product((grid_parts[0], grid_parts[1]), (table[0, :, behind], table[1, :, behind]))
     for slab in range(slabs):
         sent_b[ahead * slabs + slab] = result[slab * rows : (slab + 1) * rows]
@@ -340,15 +362,13 @@
         (limit_hbm, limit_ref), (order_hbm, order_ref), (strength_hbm, strength_ref), (mass_hbm, mass_ref),
         (twiddle_hbm, twiddle), (base_hbm, base), (back_seeds_hbm, back_seeds),
     )
-    free_sems = [n for n in range(len(later) + 1) if n != 1 + len(spans)]
-    other_loads = [load(source, target, sem) for (source, target), sem in zip(later, free_sems)]
-    seeds_load.wait()
+    other_loads = [load(source, target, n) for n, (source, target) in enumerate(later)]
 
     @pl.loop(0, quarters)
     def _(step):
         plain_step = (step + quarters - 1) // quarters
         piece = quarter_of(step) * plain_step + quarters * (1 - plain_step)
-        make_table(piece, slice(0, 2 * LANES))
+        make_table(seeds, piece, slice(0, 2 * LANES))
         keep(product((grid_parts[0], grid_parts[1]), (table[0], table[1])), piece)
 
         @pl.when(step == 0)
@@ -411,8 +431,6 @@
     blocks = LANES // fine_rows
     plain = 2 * quarters * blocks
 
-    arrivals = [quarters - 1] + list(range(quarters - 1))
-
     def back_piece(at, target, span):
         row = pl.ds(fine_rows + at, 1)
         cos_c, sin_c = back_seeds[0, row], back_seeds[1, row]
@@ -427,12 +445,12 @@
             span = pl.ds(pl.multiple_of(block * fine_rows, fine_rows), fine_rows)
             back_piece(n * blocks + block, back_table.at[n], span)
 
-    for place_of, step in enumerate(arrivals):
-        for part in range(2):
-            block = 2 * place_of + part
-            back_piece(
-                plain + 2 * quarter_of(step) + part, tail_table, slice(block * fine_rows, (block + 1) * fine_rows)
-            )
+    for target, steps in ((near_table, (0, quarters - 1)), (tail_table, range(1, quarters - 1))):
+        for place_of, step in enumerate(steps):
+            for part in range(2):
+                block = 2 * place_of + part
+                at = plain + 2 * quarter_of(step) + part
+                back_piece(at, target, slice(block * fine_rows, (block + 1) * fine_rows))
 
     sum_ref[...] = jnp.zeros_like(sum_ref)
     energy_sums[...] = jnp.zeros_like(energy_sums)
@@ -506,7 +524,7 @@
     def lev_copy(target, slot, count=1):
         return pltpu.make_async_remote_copy(
             src_ref=energy_lev.at[pl.ds(slot, count)], dst_ref=energy_lev.at[pl.ds(slot, count)],
-            send_sem=energy_sems.at[2], recv_sem=energy_sems.at[3],
+            send_sem=energy_sems.at[0], recv_sem=energy_sems.at[2],
             device_id=(target, me), device_id_type=MESH,
         )
 
@@ -517,7 +535,7 @@
         def _(step):
             wav_copy((me + step) % wav, me).start()
 
-    arrive_all(sent_c, got_c, 2, 2)
+    arrive(sent_c, got_c, 2, 2, wav - 1)
 
     @pl.loop(0, wav)
     def _(w):
@@ -529,13 +547,21 @@
     def _(w):
         back_c[w] = pack(lambda start, many: rest[w, start : start + many], wide)
 
-    arrive_all(sent_a, got_a, 0, 0)
+    arrive(sent_a, got_a, 0, 0, wav - 1)
     middle(0, got_a, back_a)
-    push_all(back_a, home_a, 3, 3)
-    arrive_all(sent_b, got_b, 1, 1)
+    sent_all(sent_a, got_a, 0)
+    push_all(back_a, home_a, 0, 3)
+    arrive(sent_b, got_b, 1, 1, wav - 1)
     middle(1, got_b, back_b)
-    push_all(back_b, home_b, 4, 4, 1)
-    push_all(back_c, home_c, 5, 4 + quarters, 1)
+    sent_all(sent_b, got_b, 1)
+    sent_all(sent_c, got_c, 2)
+    near_steps, far_steps = (0, quarters - 1), range(1, quarters - 1)
+    near_count = 2 * slabs - 1
+    push_steps(back_b, home_b, 1, 4, near_steps)
+    push_steps(back_c, home_c, 2, 5, near_steps)
+    push_steps(back_b, home_b, 1, 6, far_steps)
+    for n, step in enumerate(far_steps):
+        push_steps(back_c, home_c, 2, 7 + n, (step,))
 
     def add_pair(tile, home, steps):
         found, right = [], ([], [])
@@ -547,7 +573,7 @@
         left = halves(jnp.concatenate(found, 1))
         sum_ref[...] += product(left, [jnp.concatenate(part, 0) for part in right])
 
-    arrive_all(back_a, home_a, 3, 3)
+    arrive(back_a, home_a, 0, 3, wav - 1)
 
     @pl.loop(0, quarters, step=2)
     def _(step):
@@ -575,11 +601,6 @@
         def _():
             lev_copy(other, level).start()
 
-    for pair in range(0, quarters, 2):
-        for step in arrivals[pair : pair + 2]:
-            arrive_step(back_b, home_b, 4, 4, step)
-        add_pair(1, home_b, arrivals[pair : pair + 2])
-
     def collect_energies():
         lev_copy((level + 1) % lev, 0, lev - 1).wait()
 
@@ -589,57 +610,55 @@
         fill = jnp.zeros((8 - slabs - 1, LANES), jnp.float32)
         energy_ref[...] = jnp.concatenate(slab_sums + [total / (lev * slabs), fill], 0)
 
-    for side in range(2):
-        values = [jnp.zeros((rows, LANES), jnp.float32)] * slabs
-        for place_of in range(2 * side, 2 * side + 2):
-            if place_of == quarters - 1:
-                collect_energies()
-            arrive_step(back_c, home_c, 5, 4 + quarters, arrivals[place_of])
-            for slab in range(slabs):
-                w = quarter_of(arrivals[place_of]) * slabs + slab
-                values[slab] = values[slab] + unpack(home_c[w], quarter_starts(place_of))
+    def with_tails(values, step, place_of):
+        found = []
         for slab in range(slabs):
-            value_high, value_low = halves(values[slab])
-            at = (slice(slab * rows, (slab + 1) * rows), slice(side * LANES, (side + 1) * LANES))
-            tail_ref[(0,) + at] = value_high
-            tail_ref[(1,) + at] = value_low
-
-    for phase, (source, target) in enumerate(
-        ((sent_a, got_a), (sent_b, got_b), (sent_c, got_c), (back_a, home_a), (back_b, home_b), (back_c, home_c))
-    ):
-        batch_of(source, target, phase, 0, 0, wav - 1).wait_send()
+            value = unpack(home_c[quarter_of(step) * slabs + slab], quarter_starts(place_of))
+            found.append(value if values is None else values[slab] + value)
+        return found
+
+    arrive(back_b, home_b, 1, 4, near_count)
+    add_pair(1, home_b, near_steps)
+    arrive(back_c, home_c, 2, 5, near_count)
+    values = None
+    for place_of, step in enumerate(near_steps):
+        values = with_tails(values, step, place_of)
+    sum_ref[...] += product(halves(jnp.concatenate(values, 0)), (near_table[0], near_table[1]))
+    arrive(back_b, home_b, 1, 6, (quarters - 2) * slabs)
+    add_pair(1, home_b, far_steps)
+    sent_all(back_a, home_a, 0)
+    sent_all(back_b, home_b, 1)
+    collect_energies()
+    values = None
+    for n, step in enumerate(far_steps):
+        arrive(back_c, home_c, 2, 7 + n, slabs)
+        values = with_tails(values, step, n)
+    for slab, value in enumerate(values):
+        for part, found in enumerate(halves(value)):
+            tail_ref[part, slab * rows : (slab + 1) * rows] = found
+    sent_all(back_c, home_c, 2)
 
 
 def last_kernel(
     slabs, spans, sum_ref, tail_ref, tail_table, energy_ref, out_hbm, energies_hbm, total_hbm,
     out, energies, total, sems,
 ):
-    copies = []
-
-    def send(source, target):
-        copies.append(pltpu.make_async_copy(source, target, sems.at[len(copies)]))
-        copies[-1].start()
-
-    def ready(span):
-        return product((tail_ref[0], tail_ref[1]), (tail_table[0, :, span], tail_table[1, :, span]))
-
-    def write(span, value):
-        out[:, span] = sum_ref[:, span] + value
-        send(out.at[:, span], out_hbm.at[:, span])
-
-    held = ready(spans[0])
-    for n in range(1, len(spans)):
-        following = ready(spans[n])
-        write(spans[n - 1], held)
-        held = following
-    write(spans[-1], held)
+    for span in spans:
+        out[:, span] = sum_ref[:, span] + product(
+            (tail_ref[0], tail_ref[1]), (tail_table[0, :, span], tail_table[1, :, span])
+        )
+        pltpu.make_async_copy(out.at[:, span], out_hbm.at[:, span], sems.at[0]).start()
     sums = jnp.sum(energy_ref[...], axis=1, keepdims=True)
     for slab in range(slabs):
         energies[slab] = sums[slab, 0]
     total[0] = sums[slabs, 0]
-    send(energies, energies_hbm)
-    send(total, total_hbm)
+    copies = [
+        pltpu.make_async_copy(energies, energies_hbm, sems.at[1]),
+        pltpu.make_async_copy(total, total_hbm, sems.at[2]),
+    ]
     for copy in copies:
+        copy.start()
+    for copy in copies + [pltpu.make_async_copy(out, out_hbm, sems.at[0])]:
         copy.wait()
 
 
@@ -655,7 +674,7 @@
     columns = length // 2 // quarters
     tail = columns + 1 - LANES
     groups = LANES // tail
-    group_rows = -(-(-(-2 * rows // groups)) // 8) * 8
+    group_rows = -(-2 * rows // groups)
     padded = -(-rows // 16) * 16
     fine_rows = 32
     sizes = (slabs, rows, length, wav, lev, quarters, columns, padded, tail, groups, group_rows, fine_rows)
@@ -713,8 +732,8 @@
         functools.partial(fused_kernel, sizes),
         out_shape=(
             jax.ShapeDtypeStruct((slabs * rows, length), f32),
-            jax.ShapeDtypeStruct((2, slabs * rows, 2 * LANES), bf16),
-            jax.ShapeDtypeStruct((2, 2 * LANES, length), bf16),
+            jax.ShapeDtypeStruct((2, slabs * rows, LANES), bf16),
+            jax.ShapeDtypeStruct((2, LANES, length), bf16),
             jax.ShapeDtypeStruct((8, LANES), f32),
         ),
         in_specs=[hbm] * 9,
@@ -725,13 +744,15 @@
             pltpu.SMEM((slabs,), i32),
             pltpu.SMEM((slabs,), f32),
             pltpu.SMEM((slabs,), f32),
-            pltpu.VMEM((2, quarters + 2) + seeds.shape[2:], f32),
+            pltpu.VMEM(seeds.shape, f32),
+            pltpu.VMEM((2, 1, seeds.shape[2], LANES), f32),
             pltpu.VMEM(back_seeds.shape, f32),
             pltpu.VMEM(twiddle.shape, f32),
             pltpu.VMEM(base.shape, bf16),
             pltpu.VMEM((2, slabs * rows, length), bf16),
             pltpu.VMEM((2, length, 2 * LANES), bf16),
             pltpu.VMEM((2 * quarters, 2, LANES, length), bf16),
+            pltpu.VMEM((2, LANES, length), bf16),
             sent, sent, small, whole, whole, small, whole, whole, small, whole, whole, small,
             whole,
             pltpu.VMEM((wav, padded, LANES), f32),
@@ -739,7 +760,7 @@
             pltpu.VMEM((8, LANES), f32),
             pltpu.VMEM((wav, 1, LANES), f32),
             pltpu.VMEM((lev, 1, LANES), f32),
-            dma((8,)), dma((6,)), dma((4 + 2 * quarters,)), dma((4,)),
+            dma((7,)), dma((3,)), dma((5 + quarters,)), dma((3,)),
             pltpu.SemaphoreType.REGULAR,
         ],
         compiler_params=pltpu.CompilerParams(
@@ -769,7 +790,7 @@
             pltpu.VMEM((slabs * rows, length), f32),
             pltpu.SMEM((slabs,), f32),
             pltpu.SMEM((1,), f32),
-            dma((2 + len(spans),)),
+            dma((3,)),
         ],
         compiler_params=pltpu.CompilerParams(vmem_limit_bytes=12 * 1024 * 1024),
         name="last_product",

time: 41.2 us -> 40.8 us (level)
  no operation moved by 1% of the time
where the time goes in v4:
time: 40.8 us; the launch traced here: 40.7 us
  Pallas kernels  39.9 us (98%)
  between operations  0.8 us (2%)
    pallas_call x1, Pallas kernels, fused(): pl.pallas_call(functools.partial(fused_kernel, sizes), out_shape=(jax.Sha...  38.4 us
    pallas_call x1, Pallas kernels, fused(): pl.pallas_call(functools.partial(last_kernel, slabs, spans), out_shape=(j...  1.48 us

profile of v4, /device:TPU:1, one launch (start us, length us, event | category | flops | bytes accessed | tf_op | source)
XLA Modules:
  0.0 40.7 jit_solution(331775042126437183)
XLA Ops:
  0.6 38.4 %fused_step.1 = (f32[304,1216]{1,0:T(8,128)S(1)}, bf16[2,304,128]{2,1,0:T(8,128)(2,1)S(1)}, bf16[2,128,1216]{2,1,0:T(8,128)(2,1)S(1)}, f32[8,128]{1,0:T(8,128)S(1)}) custom-call(f32[304,1216]{1,0:T(8,128)} %bitcast.3, s32[1216]{0:T(1024)} %limit_hbm.1, s32[2]{0:T(128)} %order_hbm.1, f32[2]{0:T(128)} %strength_hbm.1, f32[2]{0:T(128)} %mass_hbm.1, ...), custom_call_target="tpu_custom_call" | custom-call | tf_op jit(solution)/shard_map/fused_step/pallas_call | solution.py:731
  39.0 1.5 %last_product.1 = (f32[304,1216]{1,0:T(8,128)}, f32[2]{0:T(128)}, f32[1]{0:T(128)}) custom-call(f32[304,1216]{1,0:T(8,128)S(1)} %get-tuple-element.10.sum_ref, bf16[2,304,128]{2,1,0:T(8,128)(2,1)S(1)} %get-tuple-element.11.tail_ref, bf16[2,128,1216]{2,1,0:T(8,128)(2,1)S(1)} %get-tuple-element.12.tail_table, f32[8,128]{1,0:T(8,128)S(1)} %get-tuple-element.13.energy_ref), custom_call_target="tpu_custom_call" | custom-call | tf_op jit(solution)/shard_map/last_product/pallas_call | solution.py:780

commit v5 on v4

--- a/solution.py
+++ b/solution.py
@@ -608,7 +608,8 @@
         for other in range(1, lev):
             total = total + energy_lev[other]
         fill = jnp.zeros((8 - slabs - 1, LANES), jnp.float32)
-        energy_ref[...] = jnp.concatenate(slab_sums + [total / (lev * slabs), fill], 0)
+        found = jnp.concatenate(slab_sums + [total / (lev * slabs), fill], 0)
+        energy_ref[...] = jnp.broadcast_to(jnp.sum(found, axis=1, keepdims=True), found.shape)
 
     def with_tails(values, step, place_of):
         found = []
@@ -643,21 +644,20 @@
     slabs, spans, sum_ref, tail_ref, tail_table, energy_ref, out_hbm, energies_hbm, total_hbm,
     out, energies, total, sems,
 ):
-    for span in spans:
-        out[:, span] = sum_ref[:, span] + product(
-            (tail_ref[0], tail_ref[1]), (tail_table[0, :, span], tail_table[1, :, span])
-        )
-        pltpu.make_async_copy(out.at[:, span], out_hbm.at[:, span], sems.at[0]).start()
-    sums = jnp.sum(energy_ref[...], axis=1, keepdims=True)
     for slab in range(slabs):
-        energies[slab] = sums[slab, 0]
-    total[0] = sums[slabs, 0]
+        energies[slab] = energy_ref[slab, 0]
+    total[0] = energy_ref[slabs, 0]
     copies = [
         pltpu.make_async_copy(energies, energies_hbm, sems.at[1]),
         pltpu.make_async_copy(total, total_hbm, sems.at[2]),
     ]
     for copy in copies:
         copy.start()
+    for span in spans:
+        out[:, span] = sum_ref[:, span] + product(
+            (tail_ref[0], tail_ref[1]), (tail_table[0, :, span], tail_table[1, :, span])
+        )
+        pltpu.make_async_copy(out.at[:, span], out_hbm.at[:, span], sems.at[0]).start()
     for copy in copies + [pltpu.make_async_copy(out, out_hbm, sems.at[0])]:
         copy.wait()
 

time: 40.8 us -> 40.9 us (level)
  no operation moved by 1% of the time
where the time goes in v5:
time: 40.9 us; the launch traced here: 40.8 us
  Pallas kernels  40 us (98%)
  between operations  0.8 us (2%)
    pallas_call x1, Pallas kernels, fused(): pl.pallas_call(functools.partial(fused_kernel, sizes), out_shape=(jax.Sha...  38.5 us
    pallas_call x1, Pallas kernels, fused(): pl.pallas_call(functools.partial(last_kernel, slabs, spans), out_shape=(j...  1.48 us

profile of v5, /device:TPU:1, one launch (start us, length us, event | category | flops | bytes accessed | tf_op | source)
XLA Modules:
  0.0 40.8 jit_solution(11426094837465902720)
XLA Ops:
  0.6 38.5 %fused_step.1 = (f32[304,1216]{1,0:T(8,128)S(1)}, bf16[2,304,128]{2,1,0:T(8,128)(2,1)S(1)}, bf16[2,128,1216]{2,1,0:T(8,128)(2,1)S(1)}, f32[8,128]{1,0:T(8,128)S(1)}) custom-call(f32[304,1216]{1,0:T(8,128)} %bitcast.3, s32[1216]{0:T(1024)} %limit_hbm.1, s32[2]{0:T(128)} %order_hbm.1, f32[2]{0:T(128)} %strength_hbm.1, f32[2]{0:T(128)} %mass_hbm.1, ...), custom_call_target="tpu_custom_call" | custom-call | tf_op jit(solution)/shard_map/fused_step/pallas_call | solution.py:731
  39.1 1.5 %last_product.1 = (f32[304,1216]{1,0:T(8,128)}, f32[2]{0:T(128)}, f32[1]{0:T(128)}) custom-call(f32[304,1216]{1,0:T(8,128)S(1)} %get-tuple-element.10.sum_ref, bf16[2,304,128]{2,1,0:T(8,128)(2,1)S(1)} %get-tuple-element.11.tail_ref, bf16[2,128,1216]{2,1,0:T(8,128)(2,1)S(1)} %get-tuple-element.12.tail_table, f32[8,128]{1,0:T(8,128)S(1)} %get-tuple-element.13.energy_ref), custom_call_target="tpu_custom_call" | custom-call | tf_op jit(solution)/shard_map/last_product/pallas_call | solution.py:780

commit v6 on v4

--- a/solution.py
+++ b/solution.py
@@ -445,7 +445,7 @@
             span = pl.ds(pl.multiple_of(block * fine_rows, fine_rows), fine_rows)
             back_piece(n * blocks + block, back_table.at[n], span)
 
-    for target, steps in ((near_table, (0, quarters - 1)), (tail_table, range(1, quarters - 1))):
+    for target, steps in ((near_table, (0, quarters - 1)), (tail_table, range(quarters - 2, 0, -1))):
         for place_of, step in enumerate(steps):
             for part in range(2):
                 block = 2 * place_of + part
@@ -555,7 +555,7 @@
     middle(1, got_b, back_b)
     sent_all(sent_b, got_b, 1)
     sent_all(sent_c, got_c, 2)
-    near_steps, far_steps = (0, quarters - 1), range(1, quarters - 1)
+    near_steps, far_steps = (0, quarters - 1), range(quarters - 2, 0, -1)
     near_count = 2 * slabs - 1
     push_steps(back_b, home_b, 1, 4, near_steps)
     push_steps(back_c, home_c, 2, 5, near_steps)

time: 40.8 us -> 40.8 us (level)
  no operation moved by 1% of the time
where the time goes in v6:
time: 40.8 us; the launch traced here: 40.7 us
  Pallas kernels  39.9 us (98%)
  between operations  0.8 us (2%)
    pallas_call x1, Pallas kernels, fused(): pl.pallas_call(functools.partial(fused_kernel, sizes), out_shape=(jax.Sha...  38.4 us
    pallas_call x1, Pallas kernels, fused(): pl.pallas_call(functools.partial(last_kernel, slabs, spans), out_shape=(j...  1.48 us

profile of v6, /device:TPU:1, one launch (start us, length us, event | category | flops | bytes accessed | tf_op | source)
XLA Modules:
  0.0 40.7 jit_solution(3202876515329763865)
XLA Ops:
  0.6 38.4 %fused_step.1 = (f32[304,1216]{1,0:T(8,128)S(1)}, bf16[2,304,128]{2,1,0:T(8,128)(2,1)S(1)}, bf16[2,128,1216]{2,1,0:T(8,128)(2,1)S(1)}, f32[8,128]{1,0:T(8,128)S(1)}) custom-call(f32[304,1216]{1,0:T(8,128)} %bitcast.3, s32[1216]{0:T(1024)} %limit_hbm.1, s32[2]{0:T(128)} %order_hbm.1, f32[2]{0:T(128)} %strength_hbm.1, f32[2]{0:T(128)} %mass_hbm.1, ...), custom_call_target="tpu_custom_call" | custom-call | tf_op jit(solution)/shard_map/fused_step/pallas_call | solution.py:731
  39.0 1.5 %last_product.1 = (f32[304,1216]{1,0:T(8,128)}, f32[2]{0:T(128)}, f32[1]{0:T(128)}) custom-call(f32[304,1216]{1,0:T(8,128)S(1)} %get-tuple-element.10.sum_ref, bf16[2,304,128]{2,1,0:T(8,128)(2,1)S(1)} %get-tuple-element.11.tail_ref, bf16[2,128,1216]{2,1,0:T(8,128)(2,1)S(1)} %get-tuple-element.12.tail_table, f32[8,128]{1,0:T(8,128)S(1)} %get-tuple-element.13.energy_ref), custom_call_target="tpu_custom_call" | custom-call | tf_op jit(solution)/shard_map/last_product/pallas_call | solution.py:780
